TPU v7x, 32 devices: a whole 2x2x4 slice. The times are simulated.
32 devices in a mesh: gx: 2 (over y), gy: 4 (over x, core), gz: 4 (over z).
Axes of the slice: x: 2, y: 2, z: 4, core: 2. Of those that a mesh axis runs over, the one named last changes fastest.
Arguments:
- rhs_velocity: float32 [3, 8, 32, 512], P(None, 'gx', 'gy', 'gz'), may hold values from -6 to 6
- rhs_pressure: float32 [8, 32, 512], P('gx', 'gy', 'gz'), may hold values from -6 to 6
- layer_ids: int32 [8, 32, 512], P('gx', 'gy', 'gz'), may hold values from 0 to 7
- visc_table: float32 [8], replicated, may hold values from 0.5 to 8
- stencil: float32 [27, 3, 3], replicated, as said below
Outputs:
- velocity_out: float32 [3, 8, 32, 512], P(None, 'gx', 'gy', 'gz')
- pressure_out: float32 [8, 32, 512], P('gx', 'gy', 'gz')
Inputs may be any that keep to these rules, and one draw needn't show every extreme that they name: The block stencil[13] has a positive diagonal that dominates its row together with all other blocks' entries.
All inputs are finite; a program needn't handle non-finite values.
Results may differ from a plain program's by a relative error of at most 0.00015.
Values sent between devices are 32-bit elements; how exact they have to be, the bound alone decides.
A program may use at most 64 MiB of HBM per device.

v0:
```python
import jax
import jax.numpy as jnp
from jax import lax
from jax.sharding import PartitionSpec as P

LOW_BOUND = 0.2
HIGH_BOUND = 1.8
OMEGA = 2.0 / 3.0


def padded_2(block, sides, width):
    for axis, dim in sides:
        count = lax.axis_size(axis)
        forward = [(i, i + 1) for i in range(count - 1)]
        backward = [(target, source) for source, target in forward]
        low = lax.ppermute(
            lax.slice_in_dim(block, block.shape[dim] - width, None, axis=dim), axis, forward
        )
        high = lax.ppermute(lax.slice_in_dim(block, 0, width, axis=dim), axis, backward)
        block = jnp.concatenate([low, block, high], axis=dim)
    return block


def cheb_consts():
    theta = (HIGH_BOUND + LOW_BOUND) / 2.0
    delta = (HIGH_BOUND - LOW_BOUND) / 2.0
    sigma = theta / delta
    rho_zero = 1.0 / sigma
    rho_one = 1.0 / (2.0 * sigma - rho_zero)
    return (theta, delta, rho_zero, rho_one)


def stencil_sum(padded, stencil):
    sizes = (padded.shape[1] - 2, padded.shape[2] - 2, padded.shape[3] - 2)
    total = jnp.zeros((3,) + sizes, jnp.float32)
    for first in range(3):
        for second in range(3):
            for third in range(3):
                slab = padded[
                    :,
                    first : first + sizes[0],
                    second : second + sizes[1],
                    third : third + sizes[2],
                ]
                block = stencil[first * 9 + second * 3 + third]
                total = total + jnp.einsum(
                    "ij,jxyz->ixyz", block, slab, precision=lax.Precision.HIGHEST
                )
    return total


def lookup(layer_ids, visc_table):
    eta = jnp.zeros(layer_ids.shape, jnp.float32)
    for layer in range(visc_table.shape[0]):
        eta = eta + jnp.where(layer_ids == layer, visc_table[layer], 0.0)
    return eta


def face_sum(padded):
    beside = padded[2:, 1:-1, 1:-1] + padded[:-2, 1:-1, 1:-1]
    beside = beside + padded[1:-1, 2:, 1:-1] + padded[1:-1, :-2, 1:-1]
    beside = beside + padded[1:-1, 1:-1, 2:] + padded[1:-1, 1:-1, :-2]
    return beside


def coarsen(field):
    shape = field.shape
    blocks = field.reshape(shape[:-3] + (shape[-3] // 2, 2, shape[-2] // 2, 2, shape[-1] // 2, 2))
    count = len(shape)
    return jnp.mean(blocks, axis=(count - 2, count, count + 2))


def refine(field):
    return jnp.repeat(jnp.repeat(jnp.repeat(field, 2, axis=1), 2, axis=2), 2, axis=3)


def fine_apply(field, eta, stencil):
    padded = padded_2(field, (("gx", 1), ("gy", 2), ("gz", 3)), 1)
    return eta[None] * stencil_sum(padded, stencil)


def on_device(rhs_velocity, rhs_pressure, layer_ids, visc_table, stencil):
    theta, delta, rho_zero, rho_one = cheb_consts()
    eta = lookup(layer_ids, visc_table)
    kc = (stencil[13, 0, 0] + stencil[13, 1, 1] + stencil[13, 2, 2]) / 3.0
    dinv = 1.0 / (eta * kc)
    weight_cheb = 2.0 * rho_one / delta
    weight = 1.0 / eta
    pinv = 1.0 / (6.0 * weight)
    first = dinv[None] * rhs_velocity / theta
    resid = rhs_velocity - fine_apply(first, eta, stencil)
    second = rho_one * rho_zero * first + weight_cheb * dinv[None] * resid
    smoothed = first + second
    residual = rhs_velocity - fine_apply(smoothed, eta, stencil)
    coarse_res = coarsen(residual)
    scale_coarse = 0.25 * coarsen(eta)
    dinv_coarse = 1.0 / (scale_coarse * kc)
    coarse_first = dinv_coarse[None] * coarse_res / theta
    coarse_pad = padded_2(coarse_first, (("gx", 1), ("gy", 2), ("gz", 3)), 1)
    coarse_resid = coarse_res - scale_coarse[None] * stencil_sum(coarse_pad, stencil)
    coarse_second = (
        rho_one * rho_zero * coarse_first + weight_cheb * dinv_coarse[None] * coarse_resid
    )
    correction = coarse_first + coarse_second
    start = smoothed + refine(correction)
    resid = rhs_velocity - fine_apply(start, eta, stencil)
    first = dinv[None] * resid / theta
    middle = start + first
    resid = rhs_velocity - fine_apply(middle, eta, stencil)
    second = rho_one * rho_zero * first + weight_cheb * dinv[None] * resid
    velocity_out = middle + second
    pressure = OMEGA * pinv * rhs_pressure
    for sweep in range(2):
        padded = padded_2(pressure, (("gx", 0), ("gy", 1), ("gz", 2)), 1)
        applied = weight * (6.0 * pressure - face_sum(padded))
        pressure = pressure + OMEGA * pinv * (rhs_pressure - applied)
    return (velocity_out, pressure)


def solution(mesh):
    placed = (P(None, "gx", "gy", "gz"), P("gx", "gy", "gz"), P("gx", "gy", "gz"), P(), P())
    return jax.shard_map(
        on_device,
        mesh=mesh,
        in_specs=placed,
        out_specs=(P(None, "gx", "gy", "gz"), P("gx", "gy", "gz")),
        check_vma=False,
    )
```

profile of v0, /device:TPU:0, one launch (start us, length us, event | category | flops | bytes accessed | tf_op | source)
XLA Modules:
  0.0 206.9 jit_solution(17718716511729512360)
XLA Ops:
  0.7 1.6 fusion.519
  2.3 5.8 %fusion.333 = (f32[4,8,128]{2,1,0:T(8,128)S(1)}, f32[4,8,128]{2,1,0:T(8,128)S(1)}) fusion(f32[4,8,128]{2,1,0:T(8,128)} %param.6, f32[]{:T(128)} %bitcast.7, s32[4,8,128]{2,1,0:T(8,128)} %param.7, f32[]{:T(128)} %bitcast.6, f32[]{:T(128)} %bitcast.5, f32[]{:T(128)} %bitcast.4, f32[]{:T(128)} %bitcast.3, f32[]{:T(128)} %bitcast.2, f32[]{:T(128)} %bitcast.1, ...), kind=kLoop, calls=%fused_computation.475 | loop fusion | flops 114688 | bytes 65568 | tf_op jit(solution)/shard_map/mul | solution.py:112
  8.1 1.3 collective-permute-start.30
  9.4 4.9 %collective-permute-start.31 = (f32[1,8,128]{2,1,0:T(8,128)S(1)}, f32[1,8,128]{2,1,0:T(8,128)S(1)}, u32[]{:S(2)}, u32[]{:S(2)}) collective-permute-start(f32[1,8,128]{2,1,0:T(8,128)S(1)} %get-tuple-element.89), channel_id=1, source_target_pairs={{0,16},{1,17},{2,18},{3,19},{4,20},{5,21},{6,22},{7,23},{8,24},{9,... | collective-permute-start | bytes 12296 | tf_op jit(solution)/shard_map/ppermute | solution.py:16
  14.3 1.4 fusion.518
  18.6 1.3 collective-permute-start
  19.9 1.3 collective-permute-start.1
  21.2 1.6 slice_reduce_fusion.1
  24.1 3.0 %collective-permute-start.33 = (f32[6,1,128]{2,1,0:T(1,128)S(1)}, f32[6,1,128]{2,1,0:T(1,128)S(1)}, u32[]{:S(2)}, u32[]{:S(2)}) collective-permute-start(f32[6,1,128]{2,1,0:T(1,128)S(1)} %get-tuple-element.85), channel_id=1, source_target_pairs={{0,4},{4,8},{8,12},{1,5},{5,9},{9,13},{2,6},{6,10},{10,14},{3,7},{... | collective-permute-start | bytes 9224 | tf_op jit(solution)/shard_map/ppermute | solution.py:16
  30.8 5.2 %collective-permute-start.35 = (f32[6,10,1]{2,1,0:T(8,128)S(1)}, f32[6,10,1]{2,1,0:T(8,128)S(1)}, u32[]{:S(2)}, u32[]{:S(2)}) collective-permute-start(f32[6,10,1]{2,1,0:T(8,128)S(1)} %get-tuple-element.76), channel_id=1, source_target_pairs={{0,1},{1,2},{2,3},{4,5},{5,6},{6,7},{8,9},{9,10},{10,11},{12,13},{... | collective-permute-start | bytes 728 | tf_op jit(solution)/shard_map/ppermute | solution.py:16
  36.2 1.7 collective-permute-done.35
  38.0 1.3 collective-permute-start.36
  39.3 4.5 %collective-permute-start.37 = (f32[1,8,128]{2,1,0:T(8,128)S(1)}, f32[1,8,128]{2,1,0:T(8,128)S(1)}, u32[]{:S(2)}, u32[]{:S(2)}) collective-permute-start(f32[1,8,128]{2,1,0:T(8,128)S(1)} %get-tuple-element.87), channel_id=1, source_target_pairs={{0,16},{1,17},{2,18},{3,19},{4,20},{5,21},{6,22},{7,23},{8,24},{9,... | collective-permute-start | bytes 12296 | tf_op jit(solution)/shard_map/ppermute | solution.py:16
  46.4 3.0 %collective-permute-start.39 = (f32[6,1,128]{2,1,0:T(1,128)S(1)}, f32[6,1,128]{2,1,0:T(1,128)S(1)}, u32[]{:S(2)}, u32[]{:S(2)}) collective-permute-start(f32[6,1,128]{2,1,0:T(1,128)S(1)} %get-tuple-element.83), channel_id=1, source_target_pairs={{0,4},{4,8},{8,12},{1,5},{5,9},{9,13},{2,6},{6,10},{10,14},{3,7},{... | collective-permute-start | bytes 9224 | tf_op jit(solution)/shard_map/ppermute | solution.py:16
  49.5 3.6 %collective-permute-start.2 = (f32[3,6,1,128]{3,0,2,1:T(4,128)S(1)}, f32[3,6,1,128]{3,0,2,1:T(4,128)S(1)}, u32[]{:S(2)}, u32[]{:S(2)}) collective-permute-start(f32[3,6,1,128]{3,0,2,1:T(4,128)S(1)} %get-tuple-element.63), channel_id=1, source_target_pairs={{0,4},{4,8},{8,12},{1,5},{5,9},{9,13},{2,6},{6,10},{10,14},{3,7},{... | collective-permute-start | bytes 27656 | tf_op jit(solution)/shard_map/ppermute | solution.py:16
  55.9 4.9 %collective-permute-start.41 = (f32[6,10,1]{2,1,0:T(8,128)S(1)}, f32[6,10,1]{2,1,0:T(8,128)S(1)}, u32[]{:S(2)}, u32[]{:S(2)}) collective-permute-start(f32[6,10,1]{2,1,0:T(8,128)S(1)} %get-tuple-element.74), channel_id=1, source_target_pairs={{0,1},{1,2},{2,3},{4,5},{5,6},{6,7},{8,9},{9,10},{10,11},{12,13},{... | collective-permute-start | bytes 728 | tf_op jit(solution)/shard_map/ppermute | solution.py:16
  61.0 1.7 collective-permute-done.41
  63.6 4.4 %collective-permute-start.4 = (f32[3,6,10,1]{3,0,2,1:T(4,128)S(1)}, f32[3,6,10,1]{3,0,2,1:T(4,128)S(1)}, u32[]{:S(2)}, u32[]{:S(2)}) collective-permute-start(f32[3,6,10,1]{3,0,2,1:T(4,128)S(1)} %get-tuple-element.55), channel_id=1, source_target_pairs={{0,1},{1,2},{2,3},{4,5},{5,6},{6,7},{8,9},{9,10},{10,11},{12,13},{... | collective-permute-start | bytes 2168 | tf_op jit(solution)/shard_map/ppermute | solution.py:16
  70.8 4.3 %collective-permute-done.5 = f32[3,6,10,1]{3,0,2,1:T(4,128)S(1)} collective-permute-done((f32[3,6,10,1]{3,0,2,1:T(4,128)S(1)}, f32[3,6,10,1]{3,0,2,1:T(4,128)S(1)}, u32[]{:S(2)}, u32[]{:S(2)}) %collective-permute-start.5) | collective-permute-done | bytes 752 | tf_op jit(solution)/shard_map/ppermute | solution.py:19
  81.4 4.2 %collective-permute-start.6 = (f32[3,1,8,128]{3,0,2,1:T(4,128)S(1)}, f32[3,1,8,128]{3,0,2,1:T(4,128)S(1)}, u32[]{:S(2)}, u32[]{:S(2)}) collective-permute-start(f32[3,1,8,128]{3,0,2,1:T(4,128)S(1)} %get-tuple-element.69), channel_id=1, source_target_pairs={{0,16},{1,17},{2,18},{3,19},{4,20},{5,21},{6,22},{7,23},{8,24},{9,... | collective-permute-start | bytes 36872 | tf_op jit(solution)/shard_map/ppermute | solution.py:16
  87.2 4.1 %collective-permute-done.7 = f32[3,1,8,128]{3,0,2,1:T(4,128)S(1)} collective-permute-done((f32[3,1,8,128]{3,0,2,1:T(4,128)S(1)}, f32[3,1,8,128]{3,0,2,1:T(4,128)S(1)}, u32[]{:S(2)}, u32[]{:S(2)}) %collective-permute-start.7) | collective-permute-done | bytes 12320 | tf_op jit(solution)/shard_map/ppermute | solution.py:19
  92.6 1.3 collective-permute-start.9
  94.1 3.7 %collective-permute-done.9 = f32[3,6,1,128]{3,0,2,1:T(4,128)S(1)} collective-permute-done((f32[3,6,1,128]{3,0,2,1:T(4,128)S(1)}, f32[3,6,1,128]{3,0,2,1:T(4,128)S(1)}, u32[]{:S(2)}, u32[]{:S(2)}) %collective-permute-start.9) | collective-permute-done | bytes 9248 | tf_op jit(solution)/shard_map/ppermute | solution.py:19
  98.0 3.9 %collective-permute-start.10 = (f32[3,6,10,1]{3,0,2,1:T(4,128)S(1)}, f32[3,6,10,1]{3,0,2,1:T(4,128)S(1)}, u32[]{:S(2)}, u32[]{:S(2)}) collective-permute-start(f32[3,6,10,1]{3,0,2,1:T(4,128)S(1)} %get-tuple-element.51), channel_id=1, source_target_pairs={{0,1},{1,2},{2,3},{4,5},{5,6},{6,7},{8,9},{9,10},{10,11},{12,13},{... | collective-permute-start | bytes 2168 | tf_op jit(solution)/shard_map/ppermute | solution.py:16
  102.0 1.5 collective-permute-start.11
  104.5 4.4 %collective-permute-done.11 = f32[3,6,10,1]{3,0,2,1:T(4,128)S(1)} collective-permute-done((f32[3,6,10,1]{3,0,2,1:T(4,128)S(1)}, f32[3,6,10,1]{3,0,2,1:T(4,128)S(1)}, u32[]{:S(2)}, u32[]{:S(2)}) %collective-permute-start.11) | collective-permute-done | bytes 752 | tf_op jit(solution)/shard_map/ppermute | solution.py:19
  115.1 3.2 %reshape.40 = f32[3,2,2,4,2,64,2]{6,5,4,3,2,1,0:T(8,128)S(1)} reshape(f32[3,4,8,128]{3,2,1,0:T(8,128)S(1)} %copy.35) | data formatting | bytes 98304 | tf_op jit(solution)/shard_map/reshape | solution.py:68
  118.6 1.6 collective-permute-start.12
  121.7 4.1 %collective-permute-done.13 = f32[3,1,4,64]{3,0,2,1:T(4,128)S(1)} collective-permute-done((f32[3,1,4,64]{3,0,2,1:T(4,128)S(1)}, f32[3,1,4,64]{3,0,2,1:T(4,128)S(1)}, u32[]{:S(2)}, u32[]{:S(2)}) %collective-permute-start.13) | collective-permute-done | bytes 3104 | tf_op jit(solution)/shard_map/ppermute | solution.py:19
  125.8 1.5 collective-permute-start.14
  128.8 3.9 %collective-permute-done.15 = f32[3,4,1,64]{3,0,2,1:T(4,128)S(1)} collective-permute-done((f32[3,4,1,64]{3,0,2,1:T(4,128)S(1)}, f32[3,4,1,64]{3,0,2,1:T(4,128)S(1)}, u32[]{:S(2)}, u32[]{:S(2)}) %collective-permute-start.15) | collective-permute-done | bytes 3104 | tf_op jit(solution)/shard_map/ppermute | solution.py:19
  132.7 3.5 %collective-permute-start.16 = (f32[3,4,6,1]{3,0,2,1:T(4,128)S(1)}, f32[3,4,6,1]{3,0,2,1:T(4,128)S(1)}, u32[]{:S(2)}, u32[]{:S(2)}) collective-permute-start(f32[3,4,6,1]{3,0,2,1:T(4,128)S(1)} %get-tuple-element.79), channel_id=1, source_target_pairs={{0,1},{1,2},{2,3},{4,5},{5,6},{6,7},{8,9},{9,10},{10,11},{12,13},{... | collective-permute-start | bytes 872 | tf_op jit(solution)/shard_map/ppermute | solution.py:16
  136.2 1.3 collective-permute-start.17
  138.2 4.0 %collective-permute-done.17 = f32[3,4,6,1]{3,0,2,1:T(4,128)S(1)} collective-permute-done((f32[3,4,6,1]{3,0,2,1:T(4,128)S(1)}, f32[3,4,6,1]{3,0,2,1:T(4,128)S(1)}, u32[]{:S(2)}, u32[]{:S(2)}) %collective-permute-start.17) | collective-permute-done | bytes 320 | tf_op jit(solution)/shard_map/ppermute | solution.py:19
  147.4 1.6 collective-permute-start.18
  150.6 4.1 %collective-permute-done.19 = f32[3,1,8,128]{3,0,2,1:T(4,128)S(1)} collective-permute-done((f32[3,1,8,128]{3,0,2,1:T(4,128)S(1)}, f32[3,1,8,128]{3,0,2,1:T(4,128)S(1)}, u32[]{:S(2)}, u32[]{:S(2)}) %collective-permute-start.19) | collective-permute-done | bytes 12320 | tf_op jit(solution)/shard_map/ppermute | solution.py:19
  154.7 1.4 collective-permute-start.20
  157.7 3.9 %collective-permute-done.21 = f32[3,6,1,128]{3,0,2,1:T(4,128)S(1)} collective-permute-done((f32[3,6,1,128]{3,0,2,1:T(4,128)S(1)}, f32[3,6,1,128]{3,0,2,1:T(4,128)S(1)}, u32[]{:S(2)}, u32[]{:S(2)}) %collective-permute-start.21) | collective-permute-done | bytes 9248 | tf_op jit(solution)/shard_map/ppermute | solution.py:19
  161.8 1.9 collective-permute-start.22
  163.7 1.5 collective-permute-start.23
  166.3 4.3 %collective-permute-done.23 = f32[3,6,10,1]{3,0,2,1:T(4,128)S(1)} collective-permute-done((f32[3,6,10,1]{3,0,2,1:T(4,128)S(1)}, f32[3,6,10,1]{3,0,2,1:T(4,128)S(1)}, u32[]{:S(2)}, u32[]{:S(2)}) %collective-permute-start.23) | collective-permute-done | bytes 752 | tf_op jit(solution)/shard_map/ppermute | solution.py:19
  176.9 1.6 collective-permute-start.24
  180.1 4.1 %collective-permute-done.25 = f32[3,1,8,128]{3,0,2,1:T(4,128)S(1)} collective-permute-done((f32[3,1,8,128]{3,0,2,1:T(4,128)S(1)}, f32[3,1,8,128]{3,0,2,1:T(4,128)S(1)}, u32[]{:S(2)}, u32[]{:S(2)}) %collective-permute-start.25) | collective-permute-done | bytes 12320 | tf_op jit(solution)/shard_map/ppermute | solution.py:19
  184.2 1.5 collective-permute-start.26
  187.2 3.8 %collective-permute-done.27 = f32[3,6,1,128]{3,0,2,1:T(4,128)S(1)} collective-permute-done((f32[3,6,1,128]{3,0,2,1:T(4,128)S(1)}, f32[3,6,1,128]{3,0,2,1:T(4,128)S(1)}, u32[]{:S(2)}, u32[]{:S(2)}) %collective-permute-start.27) | collective-permute-done | bytes 9248 | tf_op jit(solution)/shard_map/ppermute | solution.py:19
  191.2 1.9 collective-permute-start.28
  193.1 1.3 collective-permute-start.29
  195.5 4.5 %collective-permute-done.29 = f32[3,6,10,1]{3,0,2,1:T(4,128)S(1)} collective-permute-done((f32[3,6,10,1]{3,0,2,1:T(4,128)S(1)}, f32[3,6,10,1]{3,0,2,1:T(4,128)S(1)}, u32[]{:S(2)}, u32[]{:S(2)}) %collective-permute-start.29) | collective-permute-done | bytes 752 | tf_op jit(solution)/shard_map/ppermute | solution.py:19
  (234 shorter events, 62.1 us)
Async XLA Ops:
  0.6 37.3 %copy-start.2 = (f32[4,8,128]{2,1,0:T(8,128)S(1)}, f32[4,8,128]{2,1,0:T(8,128)}, u32[]{:S(2)}) copy-start(f32[4,8,128]{2,1,0:T(8,128)} %param.6) | copy-start | bytes 49156
  0.6 43.2 %copy-start = (f32[27,3,3]{0,2,1:T(4,128)S(1)}, f32[27,3,3]{0,2,1:T(4,128)}, u32[]{:S(2)}) copy-start(f32[27,3,3]{0,2,1:T(4,128)} %param.9) | copy-start | bytes 2920
  8.1 14.7 %collective-permute-start.30 = (f32[1,8,128]{2,1,0:T(8,128)S(1)}, f32[1,8,128]{2,1,0:T(8,128)S(1)}, u32[]{:S(2)}, u32[]{:S(2)}) collective-permute-start(f32[1,8,128]{2,1,0:T(8,128)S(1)} %get-tuple-element.90), channel_id=1, source_target_pairs={{16,0},{17,1},{18,2},{19,3},{20,4},{21,5},{22,6},{23,7},{24,8},{25... | collective-permute-start | bytes 12296 | tf_op jit(solution)/shard_map/ppermute | solution.py:19
  9.4 13.4 %collective-permute-start.31 = (f32[1,8,128]{2,1,0:T(8,128)S(1)}, f32[1,8,128]{2,1,0:T(8,128)S(1)}, u32[]{:S(2)}, u32[]{:S(2)}) collective-permute-start(f32[1,8,128]{2,1,0:T(8,128)S(1)} %get-tuple-element.89), channel_id=1, source_target_pairs={{0,16},{1,17},{2,18},{3,19},{4,20},{5,21},{6,22},{7,23},{8,24},{9,... | collective-permute-start | bytes 12296 | tf_op jit(solution)/shard_map/ppermute | solution.py:16
  18.6 30.9 %collective-permute-start = (f32[3,1,8,128]{3,0,2,1:T(4,128)S(1)}, f32[3,1,8,128]{3,0,2,1:T(4,128)S(1)}, u32[]{:S(2)}, u32[]{:S(2)}) collective-permute-start(f32[3,1,8,128]{3,0,2,1:T(4,128)S(1)} %get-tuple-element.71), channel_id=1, source_target_pairs={{0,16},{1,17},{2,18},{3,19},{4,20},{5,21},{6,22},{7,23},{8,24},{9,... | collective-permute-start | bytes 36872 | tf_op jit(solution)/shard_map/ppermute | solution.py:16
  19.9 29.6 %collective-permute-start.1 = (f32[3,1,8,128]{3,0,2,1:T(4,128)S(1)}, f32[3,1,8,128]{3,0,2,1:T(4,128)S(1)}, u32[]{:S(2)}, u32[]{:S(2)}) collective-permute-start(f32[3,1,8,128]{3,0,2,1:T(4,128)S(1)} %get-tuple-element.72), channel_id=1, source_target_pairs={{16,0},{17,1},{18,2},{19,3},{20,4},{21,5},{22,6},{23,7},{24,8},{25... | collective-permute-start | bytes 36872 | tf_op jit(solution)/shard_map/ppermute | solution.py:19
  22.8 6.6 %collective-permute-start.32 = (f32[6,1,128]{2,1,0:T(1,128)S(1)}, f32[6,1,128]{2,1,0:T(1,128)S(1)}, u32[]{:S(2)}, u32[]{:S(2)}) collective-permute-start(f32[6,1,128]{2,1,0:T(1,128)S(1)} %get-tuple-element.86), channel_id=1, source_target_pairs={{4,0},{8,4},{12,8},{5,1},{9,5},{13,9},{6,2},{10,6},{14,10},{7,3},{... | collective-permute-start | bytes 9224 | tf_op jit(solution)/shard_map/ppermute | solution.py:19
  24.1 5.3 %collective-permute-start.33 = (f32[6,1,128]{2,1,0:T(1,128)S(1)}, f32[6,1,128]{2,1,0:T(1,128)S(1)}, u32[]{:S(2)}, u32[]{:S(2)}) collective-permute-start(f32[6,1,128]{2,1,0:T(1,128)S(1)} %get-tuple-element.85), channel_id=1, source_target_pairs={{0,4},{4,8},{8,12},{1,5},{5,9},{9,13},{2,6},{6,10},{10,14},{3,7},{... | collective-permute-start | bytes 9224 | tf_op jit(solution)/shard_map/ppermute | solution.py:16
  29.5 6.7 %collective-permute-start.34 = (f32[6,10,1]{2,1,0:T(8,128)S(1)}, f32[6,10,1]{2,1,0:T(8,128)S(1)}, u32[]{:S(2)}, u32[]{:S(2)}) collective-permute-start(f32[6,10,1]{2,1,0:T(8,128)S(1)} %get-tuple-element.75), channel_id=1, source_target_pairs={{1,0},{2,1},{3,2},{5,4},{6,5},{7,6},{9,8},{10,9},{11,10},{13,12},{... | collective-permute-start | bytes 728 | tf_op jit(solution)/shard_map/ppermute | solution.py:19
  30.8 7.0 %collective-permute-start.35 = (f32[6,10,1]{2,1,0:T(8,128)S(1)}, f32[6,10,1]{2,1,0:T(8,128)S(1)}, u32[]{:S(2)}, u32[]{:S(2)}) collective-permute-start(f32[6,10,1]{2,1,0:T(8,128)S(1)} %get-tuple-element.76), channel_id=1, source_target_pairs={{0,1},{1,2},{2,3},{4,5},{5,6},{6,7},{8,9},{9,10},{10,11},{12,13},{... | collective-permute-start | bytes 728 | tf_op jit(solution)/shard_map/ppermute | solution.py:16
  38.0 6.1 %collective-permute-start.36 = (f32[1,8,128]{2,1,0:T(8,128)S(1)}, f32[1,8,128]{2,1,0:T(8,128)S(1)}, u32[]{:S(2)}, u32[]{:S(2)}) collective-permute-start(f32[1,8,128]{2,1,0:T(8,128)S(1)} %get-tuple-element.88), channel_id=1, source_target_pairs={{16,0},{17,1},{18,2},{19,3},{20,4},{21,5},{22,6},{23,7},{24,8},{25... | collective-permute-start | bytes 12296 | tf_op jit(solution)/shard_map/ppermute | solution.py:19
  39.3 5.9 %collective-permute-start.37 = (f32[1,8,128]{2,1,0:T(8,128)S(1)}, f32[1,8,128]{2,1,0:T(8,128)S(1)}, u32[]{:S(2)}, u32[]{:S(2)}) collective-permute-start(f32[1,8,128]{2,1,0:T(8,128)S(1)} %get-tuple-element.87), channel_id=1, source_target_pairs={{0,16},{1,17},{2,18},{3,19},{4,20},{5,21},{6,22},{7,23},{8,24},{9,... | collective-permute-start | bytes 12296 | tf_op jit(solution)/shard_map/ppermute | solution.py:16
  45.2 9.3 %collective-permute-start.38 = (f32[6,1,128]{2,1,0:T(1,128)S(1)}, f32[6,1,128]{2,1,0:T(1,128)S(1)}, u32[]{:S(2)}, u32[]{:S(2)}) collective-permute-start(f32[6,1,128]{2,1,0:T(1,128)S(1)} %get-tuple-element.84), channel_id=1, source_target_pairs={{4,0},{8,4},{12,8},{5,1},{9,5},{13,9},{6,2},{10,6},{14,10},{7,3},{... | collective-permute-start | bytes 9224 | tf_op jit(solution)/shard_map/ppermute | solution.py:19
  46.4 8.0 %collective-permute-start.39 = (f32[6,1,128]{2,1,0:T(1,128)S(1)}, f32[6,1,128]{2,1,0:T(1,128)S(1)}, u32[]{:S(2)}, u32[]{:S(2)}) collective-permute-start(f32[6,1,128]{2,1,0:T(1,128)S(1)} %get-tuple-element.83), channel_id=1, source_target_pairs={{0,4},{4,8},{8,12},{1,5},{5,9},{9,13},{2,6},{6,10},{10,14},{3,7},{... | collective-permute-start | bytes 9224 | tf_op jit(solution)/shard_map/ppermute | solution.py:16
  49.5 13.9 %collective-permute-start.2 = (f32[3,6,1,128]{3,0,2,1:T(4,128)S(1)}, f32[3,6,1,128]{3,0,2,1:T(4,128)S(1)}, u32[]{:S(2)}, u32[]{:S(2)}) collective-permute-start(f32[3,6,1,128]{3,0,2,1:T(4,128)S(1)} %get-tuple-element.63), channel_id=1, source_target_pairs={{0,4},{4,8},{8,12},{1,5},{5,9},{9,13},{2,6},{6,10},{10,14},{3,7},{... | collective-permute-start | bytes 27656 | tf_op jit(solution)/shard_map/ppermute | solution.py:16
  53.1 10.3 %collective-permute-start.3 = (f32[3,6,1,128]{3,0,2,1:T(4,128)S(1)}, f32[3,6,1,128]{3,0,2,1:T(4,128)S(1)}, u32[]{:S(2)}, u32[]{:S(2)}) collective-permute-start(f32[3,6,1,128]{3,0,2,1:T(4,128)S(1)} %get-tuple-element.64), channel_id=1, source_target_pairs={{4,0},{8,4},{12,8},{5,1},{9,5},{13,9},{6,2},{10,6},{14,10},{7,3},{... | collective-permute-start | bytes 27656 | tf_op jit(solution)/shard_map/ppermute | solution.py:19
  54.6 6.4 %collective-permute-start.40 = (f32[6,10,1]{2,1,0:T(8,128)S(1)}, f32[6,10,1]{2,1,0:T(8,128)S(1)}, u32[]{:S(2)}, u32[]{:S(2)}) collective-permute-start(f32[6,10,1]{2,1,0:T(8,128)S(1)} %get-tuple-element.73), channel_id=1, source_target_pairs={{1,0},{2,1},{3,2},{5,4},{6,5},{7,6},{9,8},{10,9},{11,10},{13,12},{... | collective-permute-start | bytes 728 | tf_op jit(solution)/shard_map/ppermute | solution.py:19
  55.9 6.8 %collective-permute-start.41 = (f32[6,10,1]{2,1,0:T(8,128)S(1)}, f32[6,10,1]{2,1,0:T(8,128)S(1)}, u32[]{:S(2)}, u32[]{:S(2)}) collective-permute-start(f32[6,10,1]{2,1,0:T(8,128)S(1)} %get-tuple-element.74), channel_id=1, source_target_pairs={{0,1},{1,2},{2,3},{4,5},{5,6},{6,7},{8,9},{9,10},{10,11},{12,13},{... | collective-permute-start | bytes 728 | tf_op jit(solution)/shard_map/ppermute | solution.py:16
  63.6 7.2 %collective-permute-start.4 = (f32[3,6,10,1]{3,0,2,1:T(4,128)S(1)}, f32[3,6,10,1]{3,0,2,1:T(4,128)S(1)}, u32[]{:S(2)}, u32[]{:S(2)}) collective-permute-start(f32[3,6,10,1]{3,0,2,1:T(4,128)S(1)} %get-tuple-element.55), channel_id=1, source_target_pairs={{0,1},{1,2},{2,3},{4,5},{5,6},{6,7},{8,9},{9,10},{10,11},{12,13},{... | collective-permute-start | bytes 2168 | tf_op jit(solution)/shard_map/ppermute | solution.py:16
  68.0 7.1 %collective-permute-start.5 = (f32[3,6,10,1]{3,0,2,1:T(4,128)S(1)}, f32[3,6,10,1]{3,0,2,1:T(4,128)S(1)}, u32[]{:S(2)}, u32[]{:S(2)}) collective-permute-start(f32[3,6,10,1]{3,0,2,1:T(4,128)S(1)} %get-tuple-element.56), channel_id=1, source_target_pairs={{1,0},{2,1},{3,2},{5,4},{6,5},{7,6},{9,8},{10,9},{11,10},{13,12},{... | collective-permute-start | bytes 2168 | tf_op jit(solution)/shard_map/ppermute | solution.py:19
  69.5 11.6 %copy-start.1 = (f32[3,4,8,128]{3,2,1,0:T(8,128)S(1)}, f32[3,4,8,128]{3,2,1,0:T(8,128)}, u32[]{:S(2)}) copy-start(f32[3,4,8,128]{3,2,1,0:T(8,128)} %param.5) | copy-start | bytes 147460
  81.4 5.7 %collective-permute-start.6 = (f32[3,1,8,128]{3,0,2,1:T(4,128)S(1)}, f32[3,1,8,128]{3,0,2,1:T(4,128)S(1)}, u32[]{:S(2)}, u32[]{:S(2)}) collective-permute-start(f32[3,1,8,128]{3,0,2,1:T(4,128)S(1)} %get-tuple-element.69), channel_id=1, source_target_pairs={{0,16},{1,17},{2,18},{3,19},{4,20},{5,21},{6,22},{7,23},{8,24},{9,... | collective-permute-start | bytes 36872 | tf_op jit(solution)/shard_map/ppermute | solution.py:16
  85.6 5.6 %collective-permute-start.7 = (f32[3,1,8,128]{3,0,2,1:T(4,128)S(1)}, f32[3,1,8,128]{3,0,2,1:T(4,128)S(1)}, u32[]{:S(2)}, u32[]{:S(2)}) collective-permute-start(f32[3,1,8,128]{3,0,2,1:T(4,128)S(1)} %get-tuple-element.70), channel_id=1, source_target_pairs={{16,0},{17,1},{18,2},{19,3},{20,4},{21,5},{22,6},{23,7},{24,8},{25... | collective-permute-start | bytes 36872 | tf_op jit(solution)/shard_map/ppermute | solution.py:19
  91.3 2.9 %collective-permute-start.8 = (f32[3,6,1,128]{3,0,2,1:T(4,128)S(1)}, f32[3,6,1,128]{3,0,2,1:T(4,128)S(1)}, u32[]{:S(2)}, u32[]{:S(2)}) collective-permute-start(f32[3,6,1,128]{3,0,2,1:T(4,128)S(1)} %get-tuple-element.61), channel_id=1, source_target_pairs={{0,4},{4,8},{8,12},{1,5},{5,9},{9,13},{2,6},{6,10},{10,14},{3,7},{... | collective-permute-start | bytes 27656 | tf_op jit(solution)/shard_map/ppermute | solution.py:16
  92.6 5.3 %collective-permute-start.9 = (f32[3,6,1,128]{3,0,2,1:T(4,128)S(1)}, f32[3,6,1,128]{3,0,2,1:T(4,128)S(1)}, u32[]{:S(2)}, u32[]{:S(2)}) collective-permute-start(f32[3,6,1,128]{3,0,2,1:T(4,128)S(1)} %get-tuple-element.62), channel_id=1, source_target_pairs={{4,0},{8,4},{12,8},{5,1},{9,5},{13,9},{6,2},{10,6},{14,10},{7,3},{... | collective-permute-start | bytes 27656 | tf_op jit(solution)/shard_map/ppermute | solution.py:19
  98.0 6.5 %collective-permute-start.10 = (f32[3,6,10,1]{3,0,2,1:T(4,128)S(1)}, f32[3,6,10,1]{3,0,2,1:T(4,128)S(1)}, u32[]{:S(2)}, u32[]{:S(2)}) collective-permute-start(f32[3,6,10,1]{3,0,2,1:T(4,128)S(1)} %get-tuple-element.51), channel_id=1, source_target_pairs={{0,1},{1,2},{2,3},{4,5},{5,6},{6,7},{8,9},{9,10},{10,11},{12,13},{... | collective-permute-start | bytes 2168 | tf_op jit(solution)/shard_map/ppermute | solution.py:16
  102.0 6.9 %collective-permute-start.11 = (f32[3,6,10,1]{3,0,2,1:T(4,128)S(1)}, f32[3,6,10,1]{3,0,2,1:T(4,128)S(1)}, u32[]{:S(2)}, u32[]{:S(2)}) collective-permute-start(f32[3,6,10,1]{3,0,2,1:T(4,128)S(1)} %get-tuple-element.52), channel_id=1, source_target_pairs={{1,0},{2,1},{3,2},{5,4},{6,5},{7,6},{9,8},{10,9},{11,10},{13,12},{... | collective-permute-start | bytes 2168 | tf_op jit(solution)/shard_map/ppermute | solution.py:19
  118.6 3.1 %collective-permute-start.12 = (f32[3,1,4,64]{3,0,2,1:T(4,128)S(1)}, f32[3,1,4,64]{3,0,2,1:T(4,128)S(1)}, u32[]{:S(2)}, u32[]{:S(2)}) collective-permute-start(f32[3,1,4,64]{3,0,2,1:T(4,128)S(1)} %get-tuple-element.91), channel_id=1, source_target_pairs={{0,16},{1,17},{2,18},{3,19},{4,20},{5,21},{6,22},{7,23},{8,24},{9,... | collective-permute-start | bytes 9224 | tf_op jit(solution)/shard_map/ppermute | solution.py:16
  120.3 5.5 %collective-permute-start.13 = (f32[3,1,4,64]{3,0,2,1:T(4,128)S(1)}, f32[3,1,4,64]{3,0,2,1:T(4,128)S(1)}, u32[]{:S(2)}, u32[]{:S(2)}) collective-permute-start(f32[3,1,4,64]{3,0,2,1:T(4,128)S(1)} %get-tuple-element.92), channel_id=1, source_target_pairs={{16,0},{17,1},{18,2},{19,3},{20,4},{21,5},{22,6},{23,7},{24,8},{25... | collective-permute-start | bytes 9224 | tf_op jit(solution)/shard_map/ppermute | solution.py:19
  125.8 3.0 %collective-permute-start.14 = (f32[3,4,1,64]{3,0,2,1:T(4,128)S(1)}, f32[3,4,1,64]{3,0,2,1:T(4,128)S(1)}, u32[]{:S(2)}, u32[]{:S(2)}) collective-permute-start(f32[3,4,1,64]{3,0,2,1:T(4,128)S(1)} %get-tuple-element.81), channel_id=1, source_target_pairs={{0,4},{4,8},{8,12},{1,5},{5,9},{9,13},{2,6},{6,10},{10,14},{3,7},{... | collective-permute-start | bytes 9224 | tf_op jit(solution)/shard_map/ppermute | solution.py:16
  127.3 5.3 %collective-permute-start.15 = (f32[3,4,1,64]{3,0,2,1:T(4,128)S(1)}, f32[3,4,1,64]{3,0,2,1:T(4,128)S(1)}, u32[]{:S(2)}, u32[]{:S(2)}) collective-permute-start(f32[3,4,1,64]{3,0,2,1:T(4,128)S(1)} %get-tuple-element.82), channel_id=1, source_target_pairs={{4,0},{8,4},{12,8},{5,1},{9,5},{13,9},{6,2},{10,6},{14,10},{7,3},{... | collective-permute-start | bytes 9224 | tf_op jit(solution)/shard_map/ppermute | solution.py:19
  132.7 5.5 %collective-permute-start.16 = (f32[3,4,6,1]{3,0,2,1:T(4,128)S(1)}, f32[3,4,6,1]{3,0,2,1:T(4,128)S(1)}, u32[]{:S(2)}, u32[]{:S(2)}) collective-permute-start(f32[3,4,6,1]{3,0,2,1:T(4,128)S(1)} %get-tuple-element.79), channel_id=1, source_target_pairs={{0,1},{1,2},{2,3},{4,5},{5,6},{6,7},{8,9},{9,10},{10,11},{12,13},{... | collective-permute-start | bytes 872 | tf_op jit(solution)/shard_map/ppermute | solution.py:16
  136.2 6.0 %collective-permute-start.17 = (f32[3,4,6,1]{3,0,2,1:T(4,128)S(1)}, f32[3,4,6,1]{3,0,2,1:T(4,128)S(1)}, u32[]{:S(2)}, u32[]{:S(2)}) collective-permute-start(f32[3,4,6,1]{3,0,2,1:T(4,128)S(1)} %get-tuple-element.80), channel_id=1, source_target_pairs={{1,0},{2,1},{3,2},{5,4},{6,5},{7,6},{9,8},{10,9},{11,10},{13,12},{... | collective-permute-start | bytes 872 | tf_op jit(solution)/shard_map/ppermute | solution.py:19
  147.4 3.2 %collective-permute-start.18 = (f32[3,1,8,128]{3,0,2,1:T(4,128)S(1)}, f32[3,1,8,128]{3,0,2,1:T(4,128)S(1)}, u32[]{:S(2)}, u32[]{:S(2)}) collective-permute-start(f32[3,1,8,128]{3,0,2,1:T(4,128)S(1)} %get-tuple-element.67), channel_id=1, source_target_pairs={{0,16},{1,17},{2,18},{3,19},{4,20},{5,21},{6,22},{7,23},{8,24},{9,... | collective-permute-start | bytes 36872 | tf_op jit(solution)/shard_map/ppermute | solution.py:16
  149.0 5.6 %collective-permute-start.19 = (f32[3,1,8,128]{3,0,2,1:T(4,128)S(1)}, f32[3,1,8,128]{3,0,2,1:T(4,128)S(1)}, u32[]{:S(2)}, u32[]{:S(2)}) collective-permute-start(f32[3,1,8,128]{3,0,2,1:T(4,128)S(1)} %get-tuple-element.68), channel_id=1, source_target_pairs={{16,0},{17,1},{18,2},{19,3},{20,4},{21,5},{22,6},{23,7},{24,8},{25... | collective-permute-start | bytes 36872 | tf_op jit(solution)/shard_map/ppermute | solution.py:19
  154.7 3.0 %collective-permute-start.20 = (f32[3,6,1,128]{3,0,2,1:T(4,128)S(1)}, f32[3,6,1,128]{3,0,2,1:T(4,128)S(1)}, u32[]{:S(2)}, u32[]{:S(2)}) collective-permute-start(f32[3,6,1,128]{3,0,2,1:T(4,128)S(1)} %get-tuple-element.59), channel_id=1, source_target_pairs={{0,4},{4,8},{8,12},{1,5},{5,9},{9,13},{2,6},{6,10},{10,14},{3,7},{... | collective-permute-start | bytes 27656 | tf_op jit(solution)/shard_map/ppermute | solution.py:16
  156.1 5.5 %collective-permute-start.21 = (f32[3,6,1,128]{3,0,2,1:T(4,128)S(1)}, f32[3,6,1,128]{3,0,2,1:T(4,128)S(1)}, u32[]{:S(2)}, u32[]{:S(2)}) collective-permute-start(f32[3,6,1,128]{3,0,2,1:T(4,128)S(1)} %get-tuple-element.60), channel_id=1, source_target_pairs={{4,0},{8,4},{12,8},{5,1},{9,5},{13,9},{6,2},{10,6},{14,10},{7,3},{... | collective-permute-start | bytes 27656 | tf_op jit(solution)/shard_map/ppermute | solution.py:19
  161.8 4.5 %collective-permute-start.22 = (f32[3,6,10,1]{3,0,2,1:T(4,128)S(1)}, f32[3,6,10,1]{3,0,2,1:T(4,128)S(1)}, u32[]{:S(2)}, u32[]{:S(2)}) collective-permute-start(f32[3,6,10,1]{3,0,2,1:T(4,128)S(1)} %get-tuple-element.47), channel_id=1, source_target_pairs={{0,1},{1,2},{2,3},{4,5},{5,6},{6,7},{8,9},{9,10},{10,11},{12,13},{... | collective-permute-start | bytes 2168 | tf_op jit(solution)/shard_map/ppermute | solution.py:16
  163.7 6.9 %collective-permute-start.23 = (f32[3,6,10,1]{3,0,2,1:T(4,128)S(1)}, f32[3,6,10,1]{3,0,2,1:T(4,128)S(1)}, u32[]{:S(2)}, u32[]{:S(2)}) collective-permute-start(f32[3,6,10,1]{3,0,2,1:T(4,128)S(1)} %get-tuple-element.48), channel_id=1, source_target_pairs={{1,0},{2,1},{3,2},{5,4},{6,5},{7,6},{9,8},{10,9},{11,10},{13,12},{... | collective-permute-start | bytes 2168 | tf_op jit(solution)/shard_map/ppermute | solution.py:19
  176.9 3.2 %collective-permute-start.24 = (f32[3,1,8,128]{3,0,2,1:T(4,128)S(1)}, f32[3,1,8,128]{3,0,2,1:T(4,128)S(1)}, u32[]{:S(2)}, u32[]{:S(2)}) collective-permute-start(f32[3,1,8,128]{3,0,2,1:T(4,128)S(1)} %get-tuple-element.65), channel_id=1, source_target_pairs={{0,16},{1,17},{2,18},{3,19},{4,20},{5,21},{6,22},{7,23},{8,24},{9,... | collective-permute-start | bytes 36872 | tf_op jit(solution)/shard_map/ppermute | solution.py:16
  178.5 5.6 %collective-permute-start.25 = (f32[3,1,8,128]{3,0,2,1:T(4,128)S(1)}, f32[3,1,8,128]{3,0,2,1:T(4,128)S(1)}, u32[]{:S(2)}, u32[]{:S(2)}) collective-permute-start(f32[3,1,8,128]{3,0,2,1:T(4,128)S(1)} %get-tuple-element.66), channel_id=1, source_target_pairs={{16,0},{17,1},{18,2},{19,3},{20,4},{21,5},{22,6},{23,7},{24,8},{25... | collective-permute-start | bytes 36872 | tf_op jit(solution)/shard_map/ppermute | solution.py:19
  184.2 3.1 %collective-permute-start.26 = (f32[3,6,1,128]{3,0,2,1:T(4,128)S(1)}, f32[3,6,1,128]{3,0,2,1:T(4,128)S(1)}, u32[]{:S(2)}, u32[]{:S(2)}) collective-permute-start(f32[3,6,1,128]{3,0,2,1:T(4,128)S(1)} %get-tuple-element.57), channel_id=1, source_target_pairs={{0,4},{4,8},{8,12},{1,5},{5,9},{9,13},{2,6},{6,10},{10,14},{3,7},{... | collective-permute-start | bytes 27656 | tf_op jit(solution)/shard_map/ppermute | solution.py:16
  185.7 5.3 %collective-permute-start.27 = (f32[3,6,1,128]{3,0,2,1:T(4,128)S(1)}, f32[3,6,1,128]{3,0,2,1:T(4,128)S(1)}, u32[]{:S(2)}, u32[]{:S(2)}) collective-permute-start(f32[3,6,1,128]{3,0,2,1:T(4,128)S(1)} %get-tuple-element.58), channel_id=1, source_target_pairs={{4,0},{8,4},{12,8},{5,1},{9,5},{13,9},{6,2},{10,6},{14,10},{7,3},{... | collective-permute-start | bytes 27656 | tf_op jit(solution)/shard_map/ppermute | solution.py:19
  191.2 4.3 %collective-permute-start.28 = (f32[3,6,10,1]{3,0,2,1:T(4,128)S(1)}, f32[3,6,10,1]{3,0,2,1:T(4,128)S(1)}, u32[]{:S(2)}, u32[]{:S(2)}) collective-permute-start(f32[3,6,10,1]{3,0,2,1:T(4,128)S(1)} %get-tuple-element.43), channel_id=1, source_target_pairs={{0,1},{1,2},{2,3},{4,5},{5,6},{6,7},{8,9},{9,10},{10,11},{12,13},{... | collective-permute-start | bytes 2168 | tf_op jit(solution)/shard_map/ppermute | solution.py:16
  193.1 6.9 %collective-permute-start.29 = (f32[3,6,10,1]{3,0,2,1:T(4,128)S(1)}, f32[3,6,10,1]{3,0,2,1:T(4,128)S(1)}, u32[]{:S(2)}, u32[]{:S(2)}) collective-permute-start(f32[3,6,10,1]{3,0,2,1:T(4,128)S(1)} %get-tuple-element.44), channel_id=1, source_target_pairs={{1,0},{2,1},{3,2},{5,4},{6,5},{7,6},{9,8},{10,9},{11,10},{13,12},{... | collective-permute-start | bytes 2168 | tf_op jit(solution)/shard_map/ppermute | solution.py:19
where the time goes:
time: 209 us; the launch traced here: 207 us
  starting transfers between devices  88.4 us (42%)
  waiting for transfers between devices  58.2 us (28%)
  matrix products  35.6 us (17%)
  local copies, waits for them, and re-layouts  11.2 us (5%)
  other arithmetic  9.08 us (4%)
  between operations  4.44 us (2%)
    ppermute x21, starting transfers between devices, padded_2(): lax.ppermute(lax.slice_in_dim(block, block.shape[dim] - width, None, axis...  60.9 us
    ppermute x21, waiting for transfers between devices, padded_2(): lax.ppermute(lax.slice_in_dim(block, 0, width, axis=dim), axis, backward)  53.1 us
    dot_general x135, matrix products, stencil_sum(): jnp.einsum('ij,jxyz->ixyz', block, slab, precision=lax.Precision.HIGHEST)  35.6 us
    ppermute x21, starting transfers between devices, padded_2(): lax.ppermute(lax.slice_in_dim(block, 0, width, axis=dim), axis, backward)  27.5 us
    mul x1, other arithmetic, on_device(): pressure = OMEGA * pinv * rhs_pressure  5.8 us
    ppermute x21, waiting for transfers between devices, padded_2(): lax.ppermute(lax.slice_in_dim(block, block.shape[dim] - width, None, axis...  5.05 us
  transfers between devices with their start and end apart: 42, of which 19 were waited for; matrix products, arithmetic and copies ran while one was open for 7% of the time, Pallas kernels for 0%

commit v1 on v0

v1 whole, which is shorter than its diff:
```python
import functools
import jax
import jax.numpy as jnp
from jax import lax
from jax.experimental import pallas as pl
from jax.experimental.pallas import tpu as pltpu
from jax.sharding import PartitionSpec as P

LOW_BOUND = 0.2
HIGH_BOUND = 1.8
OMEGA = 2.0 / 3.0
THETA = (HIGH_BOUND + LOW_BOUND) / 2.0
DELTA = (HIGH_BOUND - LOW_BOUND) / 2.0
SIGMA = THETA / DELTA
RHO_ZERO = 1.0 / SIGMA
RHO_ONE = 1.0 / (2.0 * SIGMA - RHO_ZERO)
WEIGHT = 2.0 * RHO_ONE / DELTA
KEEP = RHO_ONE * RHO_ZERO
GAIN = 1.0 + KEEP + WEIGHT * THETA

DEPTH = 3
COARSE_DEPTH = 2
EDGE = 4
OFFSETS = [
    (dx, dy, dz)
    for dx in (-1, 0, 1)
    for dy in (-1, 0, 1)
    for dz in (-1, 0, 1)
    if (dx, dy, dz) != (0, 0, 0)
]


def roll(x, shift, axis):
    return pltpu.roll(x, shift % x.shape[axis], axis)


def side(d):
    return 0 if d < 0 else 1


class Halo:
    def __init__(self, planes, comps, depth, refs):
        self.n, self.c, self.d = planes, comps, depth
        self.own, self.yp, self.zp, self.xb, self.yb, self.xyb, self.zb, self.ss, self.rs = refs

    @staticmethod
    def shapes(planes, comps, depth, rows, lanes):
        half = planes * comps // 2
        slots = -(-planes * comps * 2 * EDGE // lanes)
        f32 = jnp.float32
        return [
            pltpu.VMEM((planes, comps, rows, lanes), f32),
            pltpu.VMEM((2, half, rows, lanes), f32),
            pltpu.VMEM((slots, rows, lanes), f32),
            pltpu.VMEM((2, depth, comps, rows, lanes), f32),
            pltpu.VMEM((2, half, rows, lanes), f32),
            pltpu.VMEM((2, 2, depth * comps // 2, rows, lanes), f32),
            pltpu.VMEM((3, 3, 2, slots, rows, lanes), f32),
            pltpu.SemaphoreType.DMA((len(OFFSETS),)),
            pltpu.SemaphoreType.DMA((len(OFFSETS),)),
        ]

    def clear(self):
        for ref in (self.xb, self.yb, self.xyb, self.zb):
            ref[...] = jnp.zeros(ref.shape, ref.dtype)

    def pack(self):
        rows, lanes = self.own.shape[2:]
        row = lax.broadcasted_iota(jnp.int32, (rows, lanes), 0)
        slot = lax.broadcasted_iota(jnp.int32, (rows, lanes), 1) // (2 * EDGE)
        flat = [self.own[k, c] for k in range(self.n) for c in range(self.c)]
        for q in range(len(flat) // 2):
            even, odd = flat[2 * q], roll(flat[2 * q + 1], EDGE, 0)
            self.yp[0, q] = jnp.where(row < EDGE, even, odd)
            self.yp[1, q] = jnp.where(row < EDGE, odd, even)
        per = lanes // (2 * EDGE)
        for first in range(0, len(flat), per):
            strip = jnp.zeros((rows, lanes), jnp.float32)
            for s, v in enumerate(flat[first : first + per]):
                strip = jnp.where(slot == s, roll(v, s * 2 * EDGE + EDGE, 1), strip)
            self.zp[first // per] = strip

    def copy(self, index, me, receive):
        dx, dy, dz = OFFSETS[index]
        lo = 0 if dx < 0 else self.n - self.d
        half = self.d * self.c // 2
        rx, ry, rz = (dx, dy, dz) if receive else (-dx, -dy, -dz)
        if dz:
            src, dst = self.zp, self.zb.at[rx + 1, ry + 1, side(rz)]
        elif dx and dy:
            src = self.yp.at[side(dy), pl.ds(lo * self.c // 2, half)]
            dst = self.xyb.at[side(rx), side(ry)]
        elif dx:
            src, dst = self.own.at[pl.ds(lo, self.d)], self.xb.at[side(rx)]
        else:
            src, dst = self.yp.at[side(dy)], self.yb.at[side(ry)]
        arrival = index if receive else len(OFFSETS) - 1 - index
        return pltpu.make_async_remote_copy(
            src_ref=src,
            dst_ref=dst,
            send_sem=self.ss.at[index],
            recv_sem=self.rs.at[arrival],
            device_id=target(me, OFFSETS[index]),
            device_id_type=pl.DeviceIdType.MESH,
        )

    def send(self, me, exists):
        for index in ORDER:
            @pl.when(exists[index])
            def _():
                self.copy(index, me, False).start()

    def arrive(self, me, exists):
        for index in ORDER:
            @pl.when(exists[index])
            def _():
                self.copy(index, me, True).wait_recv()

    def drain(self, me, exists):
        for index in ORDER:
            @pl.when(exists[index])
            def _():
                self.copy(index, me, False).wait_send()

    def unpack(self, out):
        rows, lanes = self.own.shape[2:]
        row = lax.broadcasted_iota(jnp.int32, (rows, lanes), 0)
        lane = lax.broadcasted_iota(jnp.int32, (rows, lanes), 1)
        high = lane % (2 * EDGE) < EDGE
        per = lanes // (2 * EDGE)
        half = self.d * self.c // 2
        skip = (self.n - self.d) * self.c // 2
        for dx in (-1, 0, 1):
            strips = []
            for t in range(self.zp.shape[0]):
                at = [
                    jnp.where(high, self.zb[dx + 1, dy + 1, 0, t], self.zb[dx + 1, dy + 1, 1, t])
                    for dy in (-1, 0, 1)
                ]
                strips.append((at[1], jnp.where(row < EDGE, at[2], at[0])))
            first = self.n - self.d if dx < 0 else 0
            last = self.d if dx > 0 else self.n
            for k in range(first, last):
                p = k + self.d + dx * self.n
                for c in range(self.c):
                    idx = k * self.c + c
                    q = idx // 2
                    if dx == 0:
                        main, minus, plus = self.own[k, c], self.yb[0, q], self.yb[1, q]
                    else:
                        s = side(dx)
                        b = skip if dx < 0 else 0
                        main = self.xb[s, k - first, c]
                        minus, plus = self.xyb[s, 0, q - b], self.xyb[s, 1, q - b]
                    if idx % 2 == 0:
                        beside = jnp.where(row < EDGE, plus, minus)
                    else:
                        beside = roll(jnp.where(row < EDGE, minus, plus), EDGE, 0)
                    back = -((idx % per) * 2 * EDGE + EDGE)
                    mid, far = strips[idx // per]
                    out[p, c, :rows, :lanes] = main
                    out[p, c, :rows, lanes:] = roll(mid, back, 1)
                    out[p, c, rows:, :lanes] = beside
                    out[p, c, rows:, lanes:] = roll(far, back, 1)


ORDER = sorted(range(len(OFFSETS)), key=lambda i: -sum(abs(d) for d in OFFSETS[i]))


def target(me, offset):
    return {axis: at + d for (axis, at), d in zip(me.items(), offset)}


def stencil_wide(ref, p, st, step):
    rows = ref.shape[2]
    lanes = ref.shape[3]
    total = [[None] * 3 for _ in range(3)]
    for a in range(3):
        for j in range(3):
            v = ref[p + a - 1, j]
            for c, w in enumerate((roll(v, step, 1), v, roll(v, lanes - step, 1))):
                for i in range(3):
                    for b in range(3):
                        term = st[(a * 9 + b * 3 + c) * 9 + i * 3 + j] * w
                        total[i][b] = term if total[i][b] is None else total[i][b] + term
    return [
        total[i][1] + roll(total[i][0], step, 0) + roll(total[i][2], rows - step, 0)
        for i in range(3)
    ]


def stencil_own(ref, p, st):
    rows, lanes = ref.shape[2], ref.shape[3]
    total = [None] * 3
    for a in range(3):
        for j in range(3):
            v = ref[p + a - 1, j]
            for c in range(3):
                w = roll(v, (1 - c) % lanes, 1) if c != 1 else v
                w = w[:, : lanes // 2]
                for b in range(3):
                    u = (roll(w, (1 - b) % rows, 0) if b != 1 else w)[: rows // 2]
                    for i in range(3):
                        term = st[(a * 9 + b * 3 + c) * 9 + i * 3 + j] * u
                        total[i] = term if total[i] is None else total[i] + term
    return total


def kernel(sizes, rv, rp, ids, table, st, vout, pout, *scratch):
    planes, rows, lanes = ids.shape
    fine = Halo(planes, 4, DEPTH, scratch[:9])
    coarse = Halo(planes // 2, 3, COARSE_DEPTH, scratch[9:18])
    wide, smooth, cwide, middle, press, eta_ref = scratch[18:]
    me = {axis: lax.axis_index(axis) for axis in sizes}
    exists = []
    for offset in OFFSETS:
        ok = None
        for (axis, at), d in zip(me.items(), offset):
            if d:
                one = at > 0 if d < 0 else at < sizes[axis] - 1
                ok = one if ok is None else jnp.logical_and(ok, one)
        exists.append(ok)

    fine.clear()
    coarse.clear()
    barrier = pltpu.get_barrier_semaphore()
    for index in ORDER:
        @pl.when(exists[index])
        def _():
            pl.semaphore_signal(
                barrier,
                inc=1,
                device_id=target(me, OFFSETS[index]),
                device_id_type=pl.DeviceIdType.MESH,
            )

    kc = jnp.full((rows, lanes), (st[117] + st[121] + st[125]) / 3.0, jnp.float32)
    inv_kc = 1.0 / kc
    inv_wide = jnp.tile(inv_kc, (2, 2))
    for k in range(planes):
        eta = jnp.zeros((rows, lanes), jnp.float32)
        for layer in range(table.shape[0]):
            eta = jnp.where(ids[k] == layer, table[layer], eta)
        eta_ref[k] = eta
        dinv = 1.0 / (eta * kc)
        for i in range(3):
            fine.own[k, i] = dinv * rv[i, k] / THETA
        fine.own[k, 3] = (OMEGA / 6.0) * eta * rp[k]
    fine.pack()
    peers = 1
    for axis, at in me.items():
        peers = peers * (
            1 + (at > 0).astype(jnp.int32) + (at < sizes[axis] - 1).astype(jnp.int32)
        )
    pl.semaphore_wait(barrier, peers - 1)
    fine.send(me, exists)

    row = lax.broadcasted_iota(jnp.int32, (2 * rows, 2 * lanes), 0)
    lane = lax.broadcasted_iota(jnp.int32, (2 * rows, 2 * lanes), 1)
    gx, gy, gz = sizes
    has_low = {axis: (me[axis] > 0).astype(jnp.float32) for axis in sizes}
    has_high = {axis: (me[axis] < sizes[axis] - 1).astype(jnp.float32) for axis in sizes}
    mask = jnp.where(row < rows, 1.0, jnp.where(row < rows + EDGE, has_high[gy], has_low[gy]))
    mask = mask * jnp.where(
        lane < lanes, 1.0, jnp.where(lane < lanes + lanes // 2, has_high[gz], has_low[gz])
    )

    def plane_mask(x):
        inside = jnp.where(x < 0, has_low[gx], jnp.where(x >= planes, has_high[gx], 1.0))
        return mask * inside

    fine.arrive(me, exists)
    fine.unpack(wide)

    def smoothing(x):
        m = plane_mask(x)
        sums = stencil_wide(wide, x + DEPTH, st, 1)
        for i in range(3):
            smooth[x + 2, i] = (GAIN * wide[x + DEPTH, i] - (WEIGHT * inv_wide) * sums[i]) * m

    @pl.loop(-1, planes + 1)
    def _(x):
        smoothing(x)

    even_row = lax.broadcasted_iota(jnp.int32, (rows, lanes), 0) % 2 == 0
    even_lane = lax.broadcasted_iota(jnp.int32, (rows, lanes), 1) % 2 == 0

    def pair_sum(v):
        v = v + jnp.where(even_row, roll(v, rows - 1, 0), roll(v, 1, 0))
        return v + jnp.where(even_lane, roll(v, lanes - 1, 1), roll(v, 1, 1))

    @pl.loop(0, planes // 2)
    def _(h):
        parts = [None] * 3
        eta_sum = None
        for half in range(2):
            x = 2 * h + half
            eta = eta_ref[x]
            eta_sum = eta if eta_sum is None else eta_sum + eta
            sums = stencil_own(smooth, x + 2, st)
            for i in range(3):
                value = eta * ((kc * THETA) * fine.own[x, i] - sums[i])
                parts[i] = value if parts[i] is None else parts[i] + value
        dinv_c = 4.0 / (pair_sum(eta_sum) * kc * THETA)
        for i in range(3):
            coarse.own[h, i] = dinv_c * pair_sum(parts[i])

    coarse.pack()
    coarse.send(me, exists)

    smoothing(-2)
    smoothing(planes + 1)

    def star(ref, x):
        v = ref(x)
        total = ref(x - 1) + ref(x + 1)
        total = total + roll(v, 1, 0) + roll(v, 2 * rows - 1, 0)
        return total + roll(v, 1, 1) + roll(v, 2 * lanes - 1, 1)

    @pl.loop(-1, planes + 1)
    def _(x):
        near = star(lambda k: wide[k + DEPTH, 3], x)
        press[x + 1] = ((2.0 - OMEGA) * wide[x + DEPTH, 3] + (OMEGA / 6.0) * near) * plane_mask(x)

    @pl.loop(0, planes)
    def _(x):
        near = star(lambda k: press[k + 1], x)
        value = wide[x + DEPTH, 3] + (1.0 - OMEGA) * press[x + 1] + (OMEGA / 6.0) * near
        pout[x] = value[:rows, :lanes]

    coarse.arrive(me, exists)
    coarse.unpack(cwide)

    @pl.loop(-1, planes // 2 + 1)
    def _(h):
        sums = stencil_wide(cwide, h + COARSE_DEPTH, st, 2)
        m = plane_mask(2 * h)
        for i in range(3):
            value = GAIN * cwide[h + COARSE_DEPTH, i] - (WEIGHT * inv_wide) * sums[i]
            value = value * m
            smooth[2 * h + 2, i] += value
            smooth[2 * h + 3, i] += value

    @pl.loop(-1, planes + 1)
    def _(x):
        m = plane_mask(x)
        sums = stencil_wide(smooth, x + 2, st, 1)
        for i in range(3):
            first = wide[x + DEPTH, i] - (inv_wide / THETA) * sums[i]
            middle[x + 1, i] = smooth[x + 2, i] + first * m

    @pl.loop(0, planes)
    def _(x):
        sums = stencil_own(middle, x + 1, st)
        for i in range(3):
            mid = middle[x + 1, i, :rows, :lanes]
            first = mid - smooth[x + 2, i, :rows, :lanes]
            scaled = (WEIGHT * THETA) * fine.own[x, i] - (WEIGHT * inv_kc) * sums[i]
            vout[i, x] = mid + KEEP * first + scaled

    fine.drain(me, exists)
    coarse.drain(me, exists)


def on_device(sizes, rhs_velocity, rhs_pressure, layer_ids, visc_table, stencil):
    planes, rows, lanes = layer_ids.shape
    f32 = jnp.float32
    vmem = pl.BlockSpec(memory_space=pltpu.VMEM)
    smem = pl.BlockSpec(memory_space=pltpu.SMEM)
    return pl.pallas_call(
        functools.partial(kernel, sizes),
        out_shape=(
            jax.ShapeDtypeStruct(rhs_velocity.shape, f32),
            jax.ShapeDtypeStruct(rhs_pressure.shape, f32),
        ),
        in_specs=[vmem, vmem, vmem, smem, smem],
        out_specs=(vmem, vmem),
        scratch_shapes=[
            *Halo.shapes(planes, 4, DEPTH, rows, lanes),
            *Halo.shapes(planes // 2, 3, COARSE_DEPTH, rows, lanes),
            pltpu.VMEM((planes + 2 * DEPTH, 4, 2 * rows, 2 * lanes), f32),
            pltpu.VMEM((planes + 4, 3, 2 * rows, 2 * lanes), f32),
            pltpu.VMEM((planes // 2 + 2 * COARSE_DEPTH, 3, 2 * rows, 2 * lanes), f32),
            pltpu.VMEM((planes + 2, 3, 2 * rows, 2 * lanes), f32),
            pltpu.VMEM((planes + 2, 2 * rows, 2 * lanes), f32),
            pltpu.VMEM((planes, rows, lanes), f32),
        ],
        compiler_params=pltpu.CompilerParams(collective_id=0, has_side_effects=True),
        name="stokes",
    )(rhs_velocity, rhs_pressure, layer_ids, visc_table, stencil.reshape(-1))


def solution(mesh):
    placed = (P(None, "gx", "gy", "gz"), P("gx", "gy", "gz"), P("gx", "gy", "gz"), P(), P())
    sizes = {axis: mesh.shape[axis] for axis in ("gx", "gy", "gz")}
    return jax.shard_map(
        functools.partial(on_device, sizes),
        mesh=mesh,
        in_specs=placed,
        out_specs=(P(None, "gx", "gy", "gz"), P("gx", "gy", "gz")),
        check_vma=False,
    )
```

time: 209 us -> 26.9 us (0.13)
  starting transfers between devices: 88.4 us -> 0 us
  waiting for transfers between devices: 58.2 us -> 0 us
  matrix products: 35.6 us -> 0 us
  Pallas kernels: 0 us -> 22.4 us
  other arithmetic: 9.08 us -> 0 us
  local copies, waits for them, and re-layouts: 11.2 us -> 3.57 us
  between operations: 4.44 us -> 0.65 us
    ppermute x42 -> x0, starting transfers between devices: 88.4 us -> none  [the longest x21 60.9 us: padded_2(): lax.ppermute(lax.slice_in_dim(block, block.shape[dim] - width, None, axis...]
    ppermute x42 -> x0, waiting for transfers between devices: 58.2 us -> none  [the longest x21 53.1 us: padded_2(): lax.ppermute(lax.slice_in_dim(block, 0, width, axis=dim), axis, backward)]
    dot_general x135 -> x0, matrix products: 35.6 us -> none  [stencil_sum(): jnp.einsum('ij,jxyz->ixyz', block, slab, precision=lax.Precision.HIGHEST)]
    pallas_call x0 -> x1, Pallas kernels: none -> 22.4 us  [on_device(): pl.pallas_call(functools.partial(kernel, sizes), out_shape=(jax.ShapeDtyp...]
    mul x5 -> x0, other arithmetic: 6.67 us -> none  [the longest x1 5.8 us: on_device(): pressure = OMEGA * pinv * rhs_pressure]
    slice x18 -> x0, local copies, waits for them, and re-layouts: 5.61 us -> none  [the longest x2 1.83 us: stencil_sum(): block = stencil[first * 9 + second * 3 + third]]
    reshape x4 -> x1, local copies, waits for them, and re-layouts: 4.63 us -> 0.74 us  [on_device(): stencil.reshape(-1)]
    unnamed x7 -> x5, local copies, waits for them, and re-layouts: 0.64 us -> 2.84 us
  transfers between devices with their start and end apart: 42 -> 0, of which waited for: 19 -> 0; matrix products, arithmetic and copies ran while one was open for 7% -> 0% of each run, Pallas kernels for 0% -> 0%
where the time goes in v1:
time: 26.9 us; the launch traced here: 26.7 us
  Pallas kernels  22.4 us (83%)
  local copies, waits for them, and re-layouts  3.57 us (13%)
  between operations  0.65 us (2%)
    pallas_call x1, Pallas kernels, on_device(): pl.pallas_call(functools.partial(kernel, sizes), out_shape=(jax.ShapeDtyp...  22.4 us
    unnamed x5, local copies, waits for them, and re-layouts  2.84 us
    reshape x1, local copies, waits for them, and re-layouts, on_device(): stencil.reshape(-1)  0.74 us

profile of v1, /device:TPU:0, one launch (start us, length us, event | category | flops | bytes accessed | tf_op | source)
XLA Modules:
  0.0 26.7 jit_solution(11649220660475560486)
XLA Ops:
  0.6 0.8 %copy.7 = f32[27,3,3]{2,1,0:T(4,128)S(1)} copy(f32[27,3,3]{0,2,1:T(4,128)} %param.9) | data formatting | bytes 1944 | tf_op args[4]
  1.4 0.7 %reshape.7.st = f32[243]{0:T(256)} reshape(f32[27,3,3]{2,1,0:T(4,128)S(1)} %copy.7) | data formatting | bytes 1944 | tf_op jit(solution)/shard_map/reshape | solution.py:390
  2.2 22.4 %stokes.1 = (f32[3,4,8,128]{3,2,1,0:T(8,128)}, f32[4,8,128]{2,1,0:T(8,128)}) custom-call(f32[3,4,8,128]{3,2,1,0:T(8,128)} %rv.1, f32[4,8,128]{2,1,0:T(8,128)} %rp.1, s32[4,8,128]{2,1,0:T(8,128)} %ids.1, f32[8]{0:T(128)} %table.1, f32[243]{0:T(256)} %reshape.7.st), custom_call_target="tpu_custom_call" | custom-call | tf_op jit(solution)/shard_map/stokes/pallas_call | solution.py:370
  24.6 0.0 copy-start
  24.6 1.4 %copy.10 = f32[3,4,8,128]{3,2,1,0:T(8,128)} copy(f32[3,4,8,128]{3,2,1,0:T(8,128)} %get-tuple-element.4) | data formatting | bytes 98304
  26.1 0.0 copy-done
  26.1 0.6 %copy.11 = f32[4,8,128]{2,1,0:T(8,128)} copy(f32[4,8,128]{2,1,0:T(8,128)S(1)} %copy-done) | data formatting | bytes 32768
Async XLA Ops:
  24.6 1.4 %copy-start = (f32[4,8,128]{2,1,0:T(8,128)S(1)}, f32[4,8,128]{2,1,0:T(8,128)}, u32[]{:S(2)}) copy-start(f32[4,8,128]{2,1,0:T(8,128)} %get-tuple-element.5) | copy-start | bytes 49156

commit v2 on v1

--- a/solution.py
+++ b/solution.py
@@ -171,46 +171,61 @@
     return {axis: at + d for (axis, at), d in zip(me.items(), offset)}
 
 
-def stencil_wide(ref, p, st, step):
-    rows = ref.shape[2]
-    lanes = ref.shape[3]
-    total = [[None] * 3 for _ in range(3)]
-    for a in range(3):
-        for j in range(3):
-            v = ref[p + a - 1, j]
-            for c, w in enumerate((roll(v, step, 1), v, roll(v, lanes - step, 1))):
-                for i in range(3):
-                    for b in range(3):
-                        term = st[(a * 9 + b * 3 + c) * 9 + i * 3 + j] * w
-                        total[i][b] = term if total[i][b] is None else total[i][b] + term
-    return [
-        total[i][1] + roll(total[i][0], step, 0) + roll(total[i][2], rows - step, 0)
-        for i in range(3)
-    ]
-
-
-def stencil_own(ref, p, st):
-    rows, lanes = ref.shape[2], ref.shape[3]
-    total = [None] * 3
-    for a in range(3):
-        for j in range(3):
-            v = ref[p + a - 1, j]
-            for c in range(3):
-                w = roll(v, (1 - c) % lanes, 1) if c != 1 else v
-                w = w[:, : lanes // 2]
-                for b in range(3):
-                    u = (roll(w, (1 - b) % rows, 0) if b != 1 else w)[: rows // 2]
-                    for i in range(3):
-                        term = st[(a * 9 + b * 3 + c) * 9 + i * 3 + j] * u
-                        total[i] = term if total[i] is None else total[i] + term
-    return total
+def coupling(st, rows, step):
+    parts = 3 * rows
+    width = 9 * parts
+    padded = -(-width // 128) * 128
+    row = lax.broadcasted_iota(jnp.int32, (rows, padded), 0)
+    lane = lax.broadcasted_iota(jnp.int32, (rows, padded), 1)
+    head = lax.broadcasted_iota(jnp.int32, (8, padded), 1)
+    pair = (head // (3 * parts)) * 3 + (head % parts) // rows
+    low = (lane % (3 * parts)) // parts == 2
+    moved = (lane % rows - row + rows) % rows
+    bands = [moved == (step * (b - 1)) % rows for b in range(3)]
+    blocks = []
+    for c in range(3):
+        for i in range(3):
+            block = jnp.zeros((rows, padded), jnp.float32)
+            for b in range(3):
+                line = jnp.zeros((8, padded), jnp.float32)
+                for a in range(3):
+                    for j in range(3):
+                        line = jnp.where(pair == a * 3 + j, st[i, j, a * 9 + b * 3 + c], line)
+                block = jnp.where(bands[b], jnp.tile(line, (rows // 8, 1)), block)
+            high = block.astype(jnp.bfloat16).astype(jnp.float32)
+            blocks.append(jnp.where(low, block - high, high))
+    return blocks
+
+
+def put(parts, p, j, v):
+    rows = v.shape[0]
+    high = v.astype(jnp.bfloat16)
+    low = (v - high.astype(jnp.float32)).astype(jnp.bfloat16)
+    parts[p, 0, j] = high
+    parts[p, 1, j] = low
+    parts[p, 2, j] = high
+
+
+def product(matrix, parts, p):
+    depth = 3 * 9 * parts.shape[3]
+    window = parts[pl.ds(p - 1, 3)].reshape(depth, parts.shape[4])
+    return jnp.dot(matrix[:, :depth], window, preferred_element_type=jnp.float32)
+
+
+def stencil(matrix, parts, p, rows, step):
+    lanes = parts.shape[4]
+    r = product(matrix, parts, p)
+    at = lambda c, i: r[(c * 3 + i) * rows : (c * 3 + i + 1) * rows]
+    return [at(1, i) + roll(at(0, i), step, 1) + roll(at(2, i), lanes - step, 1) for i in range(3)]
 
 
 def kernel(sizes, rv, rp, ids, table, st, vout, pout, *scratch):
     planes, rows, lanes = ids.shape
     fine = Halo(planes, 4, DEPTH, scratch[:9])
     coarse = Halo(planes // 2, 3, COARSE_DEPTH, scratch[9:18])
-    wide, smooth, cwide, middle, press, eta_ref = scratch[18:]
+    wide, smooth, cwide, middle, press, eta_ref = scratch[18:24]
+    wide_p, smooth_p, cwide_p, middle_p, m_wide, m_own, m_coarse = scratch[24:]
+    tall = 2 * rows
     me = {axis: lax.axis_index(axis) for axis in sizes}
     exists = []
     for offset in OFFSETS:
@@ -234,7 +249,7 @@
                 device_id_type=pl.DeviceIdType.MESH,
             )
 
-    kc = jnp.full((rows, lanes), (st[117] + st[121] + st[125]) / 3.0, jnp.float32)
+    kc = jnp.full((rows, lanes), (st[0, 0, 13] + st[1, 1, 13] + st[2, 2, 13]) / 3.0, jnp.float32)
     inv_kc = 1.0 / kc
     inv_wide = jnp.tile(inv_kc, (2, 2))
     for k in range(planes):
@@ -255,6 +270,10 @@
     pl.semaphore_wait(barrier, peers - 1)
     fine.send(me, exists)
 
+    blocks = coupling(st, tall, 1)
+    m_wide[...] = jnp.concatenate(blocks, axis=0).astype(jnp.bfloat16)
+    m_own[...] = jnp.concatenate([b[:rows] for b in blocks], axis=0).astype(jnp.bfloat16)
+
     row = lax.broadcasted_iota(jnp.int32, (2 * rows, 2 * lanes), 0)
     lane = lax.broadcasted_iota(jnp.int32, (2 * rows, 2 * lanes), 1)
     gx, gy, gz = sizes
@@ -271,12 +290,17 @@
 
     fine.arrive(me, exists)
     fine.unpack(wide)
+    for p in range(planes + 2 * DEPTH):
+        for j in range(3):
+            put(wide_p, p, j, wide[p, j])
 
     def smoothing(x):
         m = plane_mask(x)
-        sums = stencil_wide(wide, x + DEPTH, st, 1)
-        for i in range(3):
-            smooth[x + 2, i] = (GAIN * wide[x + DEPTH, i] - (WEIGHT * inv_wide) * sums[i]) * m
+        sums = stencil(m_wide, wide_p, x + DEPTH, tall, 1)
+        for i in range(3):
+            value = (GAIN * wide[x + DEPTH, i] - (WEIGHT * inv_wide) * sums[i]) * m
+            smooth[x + 2, i] = value
+            put(smooth_p, x + 2, i, value)
 
     @pl.loop(-1, planes + 1)
     def _(x):
@@ -297,9 +321,9 @@
             x = 2 * h + half
             eta = eta_ref[x]
             eta_sum = eta if eta_sum is None else eta_sum + eta
-            sums = stencil_own(smooth, x + 2, st)
+            sums = stencil(m_own, smooth_p, x + 2, rows, 1)
             for i in range(3):
-                value = eta * ((kc * THETA) * fine.own[x, i] - sums[i])
+                value = eta * ((kc * THETA) * fine.own[x, i] - sums[i][:, :lanes])
                 parts[i] = value if parts[i] is None else parts[i] + value
         dinv_c = 4.0 / (pair_sum(eta_sum) * kc * THETA)
         for i in range(3):
@@ -308,6 +332,7 @@
     coarse.pack()
     coarse.send(me, exists)
 
+    m_coarse[...] = jnp.concatenate(coupling(st, tall, 2), axis=0).astype(jnp.bfloat16)
     smoothing(-2)
     smoothing(planes + 1)
 
@@ -330,32 +355,39 @@
 
     coarse.arrive(me, exists)
     coarse.unpack(cwide)
+    for p in range(planes // 2 + 2 * COARSE_DEPTH):
+        for j in range(3):
+            put(cwide_p, p, j, cwide[p, j])
 
     @pl.loop(-1, planes // 2 + 1)
     def _(h):
-        sums = stencil_wide(cwide, h + COARSE_DEPTH, st, 2)
+        sums = stencil(m_coarse, cwide_p, h + COARSE_DEPTH, tall, 2)
         m = plane_mask(2 * h)
         for i in range(3):
             value = GAIN * cwide[h + COARSE_DEPTH, i] - (WEIGHT * inv_wide) * sums[i]
             value = value * m
-            smooth[2 * h + 2, i] += value
-            smooth[2 * h + 3, i] += value
+            for half in range(2):
+                start = smooth[2 * h + 2 + half, i] + value
+                smooth[2 * h + 2 + half, i] = start
+                put(smooth_p, 2 * h + 2 + half, i, start)
 
     @pl.loop(-1, planes + 1)
     def _(x):
         m = plane_mask(x)
-        sums = stencil_wide(smooth, x + 2, st, 1)
+        sums = stencil(m_wide, smooth_p, x + 2, tall, 1)
         for i in range(3):
             first = wide[x + DEPTH, i] - (inv_wide / THETA) * sums[i]
-            middle[x + 1, i] = smooth[x + 2, i] + first * m
+            value = smooth[x + 2, i] + first * m
+            middle[x + 1, i] = value[:rows, :lanes]
+            put(middle_p, x + 1, i, value)
 
     @pl.loop(0, planes)
     def _(x):
-        sums = stencil_own(middle, x + 1, st)
-        for i in range(3):
-            mid = middle[x + 1, i, :rows, :lanes]
+        sums = stencil(m_own, middle_p, x + 1, rows, 1)
+        for i in range(3):
+            mid = middle[x + 1, i]
             first = mid - smooth[x + 2, i, :rows, :lanes]
-            scaled = (WEIGHT * THETA) * fine.own[x, i] - (WEIGHT * inv_kc) * sums[i]
+            scaled = (WEIGHT * THETA) * fine.own[x, i] - (WEIGHT * inv_kc) * sums[i][:, :lanes]
             vout[i, x] = mid + KEEP * first + scaled
 
     fine.drain(me, exists)
@@ -365,13 +397,14 @@
 def on_device(sizes, rhs_velocity, rhs_pressure, layer_ids, visc_table, stencil):
     planes, rows, lanes = layer_ids.shape
     f32 = jnp.float32
+    columns = -(-54 * rows // 128) * 128
     vmem = pl.BlockSpec(memory_space=pltpu.VMEM)
     smem = pl.BlockSpec(memory_space=pltpu.SMEM)
     return pl.pallas_call(
         functools.partial(kernel, sizes),
         out_shape=(
-            jax.ShapeDtypeStruct(rhs_velocity.shape, f32),
-            jax.ShapeDtypeStruct(rhs_pressure.shape, f32),
+            pltpu.VMEM(rhs_velocity.shape, f32),
+            pltpu.VMEM(rhs_pressure.shape, f32),
         ),
         in_specs=[vmem, vmem, vmem, smem, smem],
         out_specs=(vmem, vmem),
@@ -381,13 +414,25 @@
             pltpu.VMEM((planes + 2 * DEPTH, 4, 2 * rows, 2 * lanes), f32),
             pltpu.VMEM((planes + 4, 3, 2 * rows, 2 * lanes), f32),
             pltpu.VMEM((planes // 2 + 2 * COARSE_DEPTH, 3, 2 * rows, 2 * lanes), f32),
-            pltpu.VMEM((planes + 2, 3, 2 * rows, 2 * lanes), f32),
+            pltpu.VMEM((planes + 2, 3, rows, lanes), f32),
             pltpu.VMEM((planes + 2, 2 * rows, 2 * lanes), f32),
             pltpu.VMEM((planes, rows, lanes), f32),
+            *(
+                pltpu.VMEM((count, 3, 3, 2 * rows, 2 * lanes), jnp.bfloat16)
+                for count in (
+                    planes + 2 * DEPTH,
+                    planes + 4,
+                    planes // 2 + 2 * COARSE_DEPTH,
+                    planes + 2,
+                )
+            ),
+            pltpu.VMEM((18 * rows, columns), jnp.bfloat16),
+            pltpu.VMEM((9 * rows, columns), jnp.bfloat16),
+            pltpu.VMEM((18 * rows, columns), jnp.bfloat16),
         ],
         compiler_params=pltpu.CompilerParams(collective_id=0, has_side_effects=True),
         name="stokes",
-    )(rhs_velocity, rhs_pressure, layer_ids, visc_table, stencil.reshape(-1))
+    )(rhs_velocity, rhs_pressure, layer_ids, visc_table, jnp.transpose(stencil, (1, 2, 0)))
 
 
 def solution(mesh):

time: 26.9 us -> 23 us (0.86)
  local copies, waits for them, and re-layouts: 3.57 us -> 1.23 us
  Pallas kernels: 22.4 us -> 20.9 us
    unnamed x5 -> x2, local copies, waits for them, and re-layouts: 2.84 us -> 1.23 us
    pallas_call x1, Pallas kernels: 22.4 us -> 20.9 us  [on_device(): pl.pallas_call(functools.partial(kernel, sizes), out_shape=(pltpu.VMEM(rh...]
    reshape x1 -> x0, local copies, waits for them, and re-layouts: 0.74 us -> none  [on_device(): stencil.reshape(-1)]
where the time goes in v2:
time: 23 us; the launch traced here: 22.8 us
  Pallas kernels  20.9 us (91%)
  local copies, waits for them, and re-layouts  1.23 us (5%)
  between operations  0.64 us (3%)
    pallas_call x1, Pallas kernels, on_device(): pl.pallas_call(functools.partial(kernel, sizes), out_shape=(pltpu.VMEM(rh...  20.9 us
    unnamed x2, local copies, waits for them, and re-layouts  1.23 us

profile of v2, /device:TPU:0, one launch (start us, length us, event | category | flops | bytes accessed | tf_op | source)
XLA Modules:
  0.0 22.8 jit_solution(11522390279123443001)
XLA Ops:
  0.6 20.9 %stokes.1 = (f32[3,4,8,128]{3,2,1,0:T(8,128)S(1)}, f32[4,8,128]{2,1,0:T(8,128)S(1)}) custom-call(f32[3,4,8,128]{3,2,1,0:T(8,128)} %rv.1, f32[4,8,128]{2,1,0:T(8,128)} %rp.1, s32[4,8,128]{2,1,0:T(8,128)} %ids.1, f32[8]{0:T(128)} %table.1, f32[3,3,27]{2,1,0:T(4,128)} %bitcast.1), custom_call_target="tpu_custom_call" | custom-call | tf_op jit(solution)/shard_map/stokes/pallas_call | solution.py:403
  21.6 0.6 %copy.9 = f32[3,4,8,128]{3,2,1,0:T(8,128)} copy(f32[3,4,8,128]{3,2,1,0:T(8,128)S(1)} %get-tuple-element.2) | data formatting | bytes 98304
  22.2 0.6 %copy.10 = f32[4,8,128]{2,1,0:T(8,128)} copy(f32[4,8,128]{2,1,0:T(8,128)S(1)} %get-tuple-element.3) | data formatting | bytes 32768

commit v3 on v2

--- a/solution.py
+++ b/solution.py
@@ -219,12 +219,13 @@
     return [at(1, i) + roll(at(0, i), step, 1) + roll(at(2, i), lanes - step, 1) for i in range(3)]
 
 
-def kernel(sizes, rv, rp, ids, table, st, vout, pout, *scratch):
-    planes, rows, lanes = ids.shape
+def kernel(sizes, rv_in, rp_in, ids_in, table, st, vout, pout, *scratch):
+    planes, rows, lanes = ids_in.shape
     fine = Halo(planes, 4, DEPTH, scratch[:9])
     coarse = Halo(planes // 2, 3, COARSE_DEPTH, scratch[9:18])
     wide, smooth, cwide, middle, press, eta_ref = scratch[18:24]
-    wide_p, smooth_p, cwide_p, middle_p, m_wide, m_own, m_coarse = scratch[24:]
+    wide_p, smooth_p, cwide_p, middle_p, m_wide, m_own, m_coarse = scratch[24:31]
+    rv, rp, ids, in_sem = scratch[31:]
     tall = 2 * rows
     me = {axis: lax.axis_index(axis) for axis in sizes}
     exists = []
@@ -249,9 +250,21 @@
                 device_id_type=pl.DeviceIdType.MESH,
             )
 
+    loads = [
+        pltpu.make_async_copy(source, held, in_sem.at[n])
+        for n, (source, held) in enumerate(((rv_in, rv), (rp_in, rp), (ids_in, ids)))
+    ]
+    for load in loads:
+        load.start()
+    blocks = coupling(st, tall, 1)
+    m_wide[...] = jnp.concatenate(blocks, axis=0).astype(jnp.bfloat16)
+    m_own[...] = jnp.concatenate([b[:rows] for b in blocks], axis=0).astype(jnp.bfloat16)
+
     kc = jnp.full((rows, lanes), (st[0, 0, 13] + st[1, 1, 13] + st[2, 2, 13]) / 3.0, jnp.float32)
     inv_kc = 1.0 / kc
     inv_wide = jnp.tile(inv_kc, (2, 2))
+    for load in loads:
+        load.wait()
     for k in range(planes):
         eta = jnp.zeros((rows, lanes), jnp.float32)
         for layer in range(table.shape[0]):
@@ -269,10 +282,7 @@
         )
     pl.semaphore_wait(barrier, peers - 1)
     fine.send(me, exists)
-
-    blocks = coupling(st, tall, 1)
-    m_wide[...] = jnp.concatenate(blocks, axis=0).astype(jnp.bfloat16)
-    m_own[...] = jnp.concatenate([b[:rows] for b in blocks], axis=0).astype(jnp.bfloat16)
+    m_coarse[...] = jnp.concatenate(coupling(st, tall, 2), axis=0).astype(jnp.bfloat16)
 
     row = lax.broadcasted_iota(jnp.int32, (2 * rows, 2 * lanes), 0)
     lane = lax.broadcasted_iota(jnp.int32, (2 * rows, 2 * lanes), 1)
@@ -332,7 +342,6 @@
     coarse.pack()
     coarse.send(me, exists)
 
-    m_coarse[...] = jnp.concatenate(coupling(st, tall, 2), axis=0).astype(jnp.bfloat16)
     smoothing(-2)
     smoothing(planes + 1)
 
@@ -394,19 +403,29 @@
     coarse.drain(me, exists)
 
 
+def write_out(v, p, vout, pout, sem):
+    first = pltpu.make_async_copy(v, vout, sem.at[0])
+    second = pltpu.make_async_copy(p, pout, sem.at[1])
+    first.start()
+    second.start()
+    first.wait()
+    second.wait()
+
+
 def on_device(sizes, rhs_velocity, rhs_pressure, layer_ids, visc_table, stencil):
     planes, rows, lanes = layer_ids.shape
     f32 = jnp.float32
     columns = -(-54 * rows // 128) * 128
     vmem = pl.BlockSpec(memory_space=pltpu.VMEM)
+    hbm = pl.BlockSpec(memory_space=pl.ANY)
     smem = pl.BlockSpec(memory_space=pltpu.SMEM)
-    return pl.pallas_call(
+    results = pl.pallas_call(
         functools.partial(kernel, sizes),
         out_shape=(
             pltpu.VMEM(rhs_velocity.shape, f32),
             pltpu.VMEM(rhs_pressure.shape, f32),
         ),
-        in_specs=[vmem, vmem, vmem, smem, smem],
+        in_specs=[hbm, hbm, hbm, smem, smem],
         out_specs=(vmem, vmem),
         scratch_shapes=[
             *Halo.shapes(planes, 4, DEPTH, rows, lanes),
@@ -429,10 +448,23 @@
             pltpu.VMEM((18 * rows, columns), jnp.bfloat16),
             pltpu.VMEM((9 * rows, columns), jnp.bfloat16),
             pltpu.VMEM((18 * rows, columns), jnp.bfloat16),
+            pltpu.VMEM(rhs_velocity.shape, f32),
+            pltpu.VMEM(rhs_pressure.shape, f32),
+            pltpu.VMEM(layer_ids.shape, layer_ids.dtype),
+            pltpu.SemaphoreType.DMA((3,)),
         ],
         compiler_params=pltpu.CompilerParams(collective_id=0, has_side_effects=True),
         name="stokes",
     )(rhs_velocity, rhs_pressure, layer_ids, visc_table, jnp.transpose(stencil, (1, 2, 0)))
+    return pl.pallas_call(
+        write_out,
+        out_shape=tuple(jax.ShapeDtypeStruct(r.shape, f32) for r in results),
+        in_specs=[hbm, hbm],
+        out_specs=(hbm, hbm),
+        scratch_shapes=[pltpu.SemaphoreType.DMA((2,))],
+        compiler_params=pltpu.CompilerParams(vmem_limit_bytes=1 << 20),
+        name="write_out",
+    )(*results)
 
 
 def solution(mesh):

time: 23 us -> 22.1 us (0.961)
  local copies, waits for them, and re-layouts: 1.23 us -> 0 us
  Pallas kernels: 20.9 us -> 21.3 us
    unnamed x2 -> x0, local copies, waits for them, and re-layouts: 1.23 us -> none
    pallas_call x0 -> x1, Pallas kernels: none -> 0.64 us  [on_device(): pl.pallas_call(write_out, out_shape=tuple((jax.ShapeDtypeStruct(r.shape,...]
    pallas_call x1, Pallas kernels: 20.9 us -> 20.6 us  [on_device(): pl.pallas_call(functools.partial(kernel, sizes), out_shape=(pltpu.VMEM(rh...]
where the time goes in v3:
time: 22.1 us; the launch traced here: 21.9 us
  Pallas kernels  21.3 us (96%)
  between operations  0.64 us (3%)
    pallas_call x1, Pallas kernels, on_device(): pl.pallas_call(functools.partial(kernel, sizes), out_shape=(pltpu.VMEM(rh...  20.6 us
    pallas_call x1, Pallas kernels, on_device(): pl.pallas_call(write_out, out_shape=tuple((jax.ShapeDtypeStruct(r.shape,...  0.64 us

profile of v3, /device:TPU:0, one launch (start us, length us, event | category | flops | bytes accessed | tf_op | source)
XLA Modules:
  0.0 21.9 jit_solution(13481117607396245200)
XLA Ops:
  0.6 20.6 %stokes.1 = (f32[3,4,8,128]{3,2,1,0:T(8,128)S(1)}, f32[4,8,128]{2,1,0:T(8,128)S(1)}) custom-call(f32[3,4,8,128]{3,2,1,0:T(8,128)} %rv_in.1, f32[4,8,128]{2,1,0:T(8,128)} %rp_in.1, s32[4,8,128]{2,1,0:T(8,128)} %ids_in.1, f32[8]{0:T(128)} %table.1, f32[3,3,27]{2,1,0:T(4,128)} %bitcast.1), custom_call_target="tpu_custom_call" | custom-call | tf_op jit(solution)/shard_map/stokes/pallas_call | solution.py:422
  21.3 0.6 %write_out.1 = (f32[3,4,8,128]{3,2,1,0:T(8,128)}, f32[4,8,128]{2,1,0:T(8,128)}) custom-call(f32[3,4,8,128]{3,2,1,0:T(8,128)S(1)} %get-tuple-element.4.v, f32[4,8,128]{2,1,0:T(8,128)S(1)} %get-tuple-element.5.p), custom_call_target="tpu_custom_call" | custom-call | tf_op jit(solution)/shard_map/write_out/pallas_call | solution.py:459

commit v4 on v3

--- a/solution.py
+++ b/solution.py
@@ -312,7 +312,7 @@
             smooth[x + 2, i] = value
             put(smooth_p, x + 2, i, value)
 
-    @pl.loop(-1, planes + 1)
+    @pl.loop(-1, planes + 1, unroll=True)
     def _(x):
         smoothing(x)
 
@@ -323,7 +323,7 @@
         v = v + jnp.where(even_row, roll(v, rows - 1, 0), roll(v, 1, 0))
         return v + jnp.where(even_lane, roll(v, lanes - 1, 1), roll(v, 1, 1))
 
-    @pl.loop(0, planes // 2)
+    @pl.loop(0, planes // 2, unroll=True)
     def _(h):
         parts = [None] * 3
         eta_sum = None
@@ -351,12 +351,12 @@
         total = total + roll(v, 1, 0) + roll(v, 2 * rows - 1, 0)
         return total + roll(v, 1, 1) + roll(v, 2 * lanes - 1, 1)
 
-    @pl.loop(-1, planes + 1)
+    @pl.loop(-1, planes + 1, unroll=True)
     def _(x):
         near = star(lambda k: wide[k + DEPTH, 3], x)
         press[x + 1] = ((2.0 - OMEGA) * wide[x + DEPTH, 3] + (OMEGA / 6.0) * near) * plane_mask(x)
 
-    @pl.loop(0, planes)
+    @pl.loop(0, planes, unroll=True)
     def _(x):
         near = star(lambda k: press[k + 1], x)
         value = wide[x + DEPTH, 3] + (1.0 - OMEGA) * press[x + 1] + (OMEGA / 6.0) * near
@@ -368,7 +368,7 @@
         for j in range(3):
             put(cwide_p, p, j, cwide[p, j])
 
-    @pl.loop(-1, planes // 2 + 1)
+    @pl.loop(-1, planes // 2 + 1, unroll=True)
     def _(h):
         sums = stencil(m_coarse, cwide_p, h + COARSE_DEPTH, tall, 2)
         m = plane_mask(2 * h)
@@ -380,7 +380,7 @@
                 smooth[2 * h + 2 + half, i] = start
                 put(smooth_p, 2 * h + 2 + half, i, start)
 
-    @pl.loop(-1, planes + 1)
+    @pl.loop(-1, planes + 1, unroll=True)
     def _(x):
         m = plane_mask(x)
         sums = stencil(m_wide, smooth_p, x + 2, tall, 1)
@@ -390,7 +390,7 @@
             middle[x + 1, i] = value[:rows, :lanes]
             put(middle_p, x + 1, i, value)
 
-    @pl.loop(0, planes)
+    @pl.loop(0, planes, unroll=True)
     def _(x):
         sums = stencil(m_own, middle_p, x + 1, rows, 1)
         for i in range(3):

time: 22.1 us -> 17.6 us (0.80)
  Pallas kernels: 21.3 us -> 16.8 us
    pallas_call x1, Pallas kernels: 20.6 us -> 16.1 us  [on_device(): pl.pallas_call(functools.partial(kernel, sizes), out_shape=(pltpu.VMEM(rh...]
where the time goes in v4:
time: 17.6 us; the launch traced here: 17.4 us
  Pallas kernels  16.8 us (95%)
  between operations  0.64 us (4%)
    pallas_call x1, Pallas kernels, on_device(): pl.pallas_call(functools.partial(kernel, sizes), out_shape=(pltpu.VMEM(rh...  16.1 us
    pallas_call x1, Pallas kernels, on_device(): pl.pallas_call(write_out, out_shape=tuple((jax.ShapeDtypeStruct(r.shape,...  0.64 us

profile of v4, /device:TPU:0, one launch (start us, length us, event | category | flops | bytes accessed | tf_op | source)
XLA Modules:
  0.0 17.4 jit_solution(583767478828953058)
XLA Ops:
  0.6 16.1 %stokes.1 = (f32[3,4,8,128]{3,2,1,0:T(8,128)S(1)}, f32[4,8,128]{2,1,0:T(8,128)S(1)}) custom-call(f32[3,4,8,128]{3,2,1,0:T(8,128)} %rv_in.1, f32[4,8,128]{2,1,0:T(8,128)} %rp_in.1, s32[4,8,128]{2,1,0:T(8,128)} %ids_in.1, f32[8]{0:T(128)} %table.1, f32[3,3,27]{2,1,0:T(4,128)} %bitcast.1), custom_call_target="tpu_custom_call" | custom-call | tf_op jit(solution)/shard_map/stokes/pallas_call | solution.py:422
  16.8 0.6 %write_out.1 = (f32[3,4,8,128]{3,2,1,0:T(8,128)}, f32[4,8,128]{2,1,0:T(8,128)}) custom-call(f32[3,4,8,128]{3,2,1,0:T(8,128)S(1)} %get-tuple-element.4.v, f32[4,8,128]{2,1,0:T(8,128)S(1)} %get-tuple-element.5.p), custom_call_target="tpu_custom_call" | custom-call | tf_op jit(solution)/shard_map/write_out/pallas_call | solution.py:459
